TPU v7x, 8 devices: a whole 2x2x1 slice. The times are simulated.
8 devices in a mesh: fsdp: 2 (over z, y), ep: 4 (over x, core).
Axes of the slice: x: 2, y: 2, z: 1, core: 2. Of those that a mesh axis runs over, the one named last changes fastest.
Arguments:
- x_tok: bfloat16 [32768, 1024], P(('fsdp', 'ep'))
- dy_tok: bfloat16 [32768, 1024], P(('fsdp', 'ep'))
- expert_idx: int32 [32768, 6], P(('fsdp', 'ep'))
- gate_val: float32 [32768, 6], P(('fsdp', 'ep'))
- w_one: bfloat16 [64, 1024, 704], P('ep', 'fsdp')
- w_two: bfloat16 [64, 704, 1024], P('ep', None, 'fsdp')
- w_three: bfloat16 [64, 1024, 704], P('ep', 'fsdp')
- ws_one: bfloat16 [1024, 1408], P('fsdp')
- ws_two: bfloat16 [1408, 1024], P(None, 'fsdp')
- ws_three: bfloat16 [1024, 1408], P('fsdp')
Outputs:
- output 1: bfloat16 [32768, 1024], P(('fsdp', 'ep'))
- output 2: float32 [32768, 6], P(('fsdp', 'ep'))
- output 3: float32 [64, 1024, 704], P('ep', 'fsdp')
- output 4: float32 [64, 704, 1024], P('ep', None, 'fsdp')
- output 5: float32 [64, 1024, 704], P('ep', 'fsdp')
- output 6: float32 [1024, 1408], P('fsdp')
- output 7: float32 [1408, 1024], P(None, 'fsdp')
- output 8: float32 [1024, 1408], P('fsdp')
All inputs are finite; a program needn't handle non-finite values.
Results may differ from a plain program's by a relative error of at most 0.00527379.
Values are sent between devices in bfloat16 or wider.
A program may use at most 1 GiB of HBM per device.

v0:
```python
import jax
import jax.numpy as jnp
from jax import lax
from jax.sharding import PartitionSpec as P

CAP_NUM = 5
CAP_DEN = 4


def capacity_for(tok_dev, top_k, n_exp):
    needed = -(-(tok_dev * top_k * CAP_NUM) // (CAP_DEN * n_exp))
    return max(8, -(-needed // 8) * 8)


def route_slots(ids_dev, n_exp, capacity):
    flat_ids = ids_dev.reshape(-1)
    n_assign = flat_ids.shape[0]
    onehot = (flat_ids[:, None] == jnp.arange(n_exp, dtype=jnp.int32)[None, :]).astype(jnp.int32)
    slot_pos = jnp.sum(jnp.cumsum(onehot, axis=0) * onehot, axis=1) - 1
    slot_idx = jnp.where(slot_pos < capacity, flat_ids * capacity + slot_pos, n_exp * capacity)
    filled = jnp.full((n_exp * capacity + 1,), n_assign, jnp.int32)
    filled = filled.at[slot_idx].set(jnp.arange(n_assign, dtype=jnp.int32))
    return slot_idx, filled[: n_exp * capacity]


def swiglu_backward(x_rows, g_rows, w_a, w_b, w_c, lead_dims, batch_dim):
    up_form = lead_dims + "d," + batch_dim + "df->" + lead_dims + "f"
    back_form = lead_dims + "d," + batch_dim + "fd->" + lead_dims + "f"
    into_form = lead_dims + "f," + batch_dim + "df->" + lead_dims + "d"
    grad_in = lead_dims + "d," + lead_dims + "f->" + batch_dim + "df"
    grad_out = lead_dims + "f," + lead_dims + "d->" + batch_dim + "fd"
    h_one = jnp.einsum(up_form, x_rows, w_a, preferred_element_type=jnp.float32)
    h_three = jnp.einsum(up_form, x_rows, w_c, preferred_element_type=jnp.float32)
    sig_one = jax.nn.sigmoid(h_one)
    silu_one = h_one * sig_one
    act_rows = (silu_one * h_three).astype(jnp.bfloat16)
    d_act = jnp.einsum(back_form, g_rows, w_b, preferred_element_type=jnp.float32)
    dh_one = (d_act * h_three * sig_one * (1.0 + h_one * (1.0 - sig_one))).astype(jnp.bfloat16)
    dh_three = (d_act * silu_one).astype(jnp.bfloat16)
    dx_rows = (jnp.einsum(into_form, dh_one, w_a, preferred_element_type=jnp.float32) + jnp.einsum(into_form, dh_three, w_c, preferred_element_type=jnp.float32)).astype(jnp.bfloat16)
    dw_a = jnp.einsum(grad_in, x_rows, dh_one, preferred_element_type=jnp.float32)
    dw_b = jnp.einsum(grad_out, act_rows, g_rows, preferred_element_type=jnp.float32)
    dw_c = jnp.einsum(grad_in, x_rows, dh_three, preferred_element_type=jnp.float32)
    return dx_rows, act_rows, dw_a, dw_b, dw_c


def solution(mesh):
    ep_size = mesh.shape["ep"]
    tok_spec = P(("fsdp", "ep"), None)
    in_specs = (tok_spec, tok_spec, tok_spec, tok_spec, P("ep", "fsdp", None), P("ep", None, "fsdp"), P("ep", "fsdp", None), P("fsdp", None), P(None, "fsdp"), P("fsdp", None))
    out_specs = (tok_spec, tok_spec, P("ep", "fsdp", None), P("ep", None, "fsdp"), P("ep", "fsdp", None), P("fsdp", None), P(None, "fsdp"), P("fsdp", None))

    def device_step(x_loc, dy_loc, ids_loc, gate_loc, w_one, w_two, w_three, ws_one, ws_two, ws_three):
        tok_dev, top_k = ids_loc.shape
        model_dim = x_loc.shape[1]
        n_local = w_one.shape[0]
        n_exp = n_local * ep_size
        capacity = capacity_for(tok_dev, top_k, n_exp)
        slot_idx, filled = route_slots(ids_loc, n_exp, capacity)
        zero_row = jnp.zeros((1, model_dim), jnp.bfloat16)
        zero_one = jnp.zeros((1,), jnp.float32)
        tok_src = filled // top_k
        buf_shape = (ep_size, n_local, capacity, model_dim)
        x_send = jnp.concatenate([x_loc, zero_row])[tok_src].reshape(buf_shape)
        dy_send = jnp.concatenate([dy_loc, zero_row])[tok_src].reshape(buf_shape)
        gate_send = jnp.concatenate([gate_loc.reshape(-1), zero_one])[filled].reshape(buf_shape[:3])
        x_recv = lax.all_to_all(x_send, "ep", 0, 0, tiled=True)
        dy_recv = lax.all_to_all(dy_send, "ep", 0, 0, tiled=True)
        gate_recv = lax.all_to_all(gate_send, "ep", 0, 0, tiled=True)
        w_one_full = lax.all_gather(w_one, "fsdp", axis=1, tiled=True)
        w_three_full = lax.all_gather(w_three, "fsdp", axis=1, tiled=True)
        w_two_full = lax.all_gather(w_two, "fsdp", axis=2, tiled=True)
        ws_one_full = lax.all_gather(ws_one, "fsdp", axis=0, tiled=True)
        ws_three_full = lax.all_gather(ws_three, "fsdp", axis=0, tiled=True)
        ws_two_full = lax.all_gather(ws_two, "fsdp", axis=1, tiled=True)
        dy_wide = dy_recv.astype(jnp.float32)
        g_recv = (gate_recv[..., None] * dy_wide).astype(jnp.bfloat16)
        dx_recv, act_recv, dw_one, dw_two, dw_three = swiglu_backward(x_recv, g_recv, w_one_full, w_two_full, w_three_full, "sec", "e")
        y_recv = jnp.einsum("secf,efd->secd", act_recv, w_two_full, preferred_element_type=jnp.float32)
        dgate_recv = jnp.sum(dy_wide * y_recv, axis=-1)
        dx_back = lax.all_to_all(dx_recv, "ep", 0, 0, tiled=True).reshape(n_exp * capacity, model_dim)
        dgate_back = lax.all_to_all(dgate_recv, "ep", 0, 0, tiled=True).reshape(-1)
        dx_assign = jnp.concatenate([dx_back, zero_row])[slot_idx].reshape(tok_dev, top_k, model_dim)
        dgate_loc = jnp.concatenate([dgate_back, zero_one])[slot_idx].reshape(tok_dev, top_k)
        shared_out = swiglu_backward(x_loc, dy_loc, ws_one_full, ws_two_full, ws_three_full, "t", "")
        dx_loc = (jnp.sum(dx_assign.astype(jnp.float32), axis=1) + shared_out[0].astype(jnp.float32)).astype(jnp.bfloat16)
        dw_one = lax.psum_scatter(dw_one, "fsdp", scatter_dimension=1, tiled=True)
        dw_three = lax.psum_scatter(dw_three, "fsdp", scatter_dimension=1, tiled=True)
        dw_two = lax.psum_scatter(dw_two, "fsdp", scatter_dimension=2, tiled=True)
        dws_one = lax.psum(lax.psum_scatter(shared_out[2], "fsdp", scatter_dimension=0, tiled=True), "ep")
        dws_two = lax.psum(lax.psum_scatter(shared_out[3], "fsdp", scatter_dimension=1, tiled=True), "ep")
        dws_three = lax.psum(lax.psum_scatter(shared_out[4], "fsdp", scatter_dimension=0, tiled=True), "ep")
        return dx_loc, dgate_loc, dw_one, dw_two, dw_three, dws_one, dws_two, dws_three

    return jax.shard_map(device_step, mesh=mesh, in_specs=in_specs, out_specs=out_specs, check_vma=False)
```

profile of v0, /device:TPU:0, one launch (start us, length us, event | category | flops | bytes accessed | tf_op | source)
XLA Modules:
  0.0 4224.6 jit_solution(6014676162669529754)
XLA Ops:
  9.4 42.1 all-gather.15.cloned.1.call-done
  51.5 19.5 fusion.54
  71.0 21.2 all-gather.17.cloned.1.call-done
  92.2 19.5 fusion.55
  111.7 21.2 all-gather.13.cloned.1.call-done
  132.9 33.9 multiply_convert_fusion.1
  166.9 19.7 convolution_bitcast_fusion.1
  191.9 3.4 copy-done
  196.4 8.4 broadcast_add_fusion
  204.8 8.6 copy.79
  214.0 1.8 mul.71
  215.8 6.9 fusion.45
  222.8 19.9 convolution_bitcast_fusion
  245.2 90.3 %scatter_custom_fusion = s32[30721]{0:T(1024)S(1)} fusion(s32[24576]{0:T(1024)S(1)} %bitcast.134, s32[24576]{0:T(1024)S(1)} %iota.11, s32[]{:T(128)} %constant.15.clone.1), kind=kCustom, calls=%fused_computation.86 | custom fusion | bytes 122888 | tf_op jit(solution)/shard_map/scatter | solution.py:22
  335.6 169.3 %gather_fusion = f32[30720]{0:T(1024)S(1)} fusion(f32[24577]{0:T(1024)S(1)} %pad_maximum_fusion.1, s32[30720]{0:T(1024)S(1)} %get-tuple-element.56), kind=kCustom, calls=%fused_computation | custom fusion | bytes 368640 | tf_op jit(solution)/shard_map/gather | solution.py:66
  505.7 3.9 all-to-all-start
  509.6 7.8 concatenate.17
  517.4 154.2 %gather_fusion.2 = bf16[30720,1024]{1,0:T(8,128)(2,1)} fusion(bf16[4097,1024]{1,0:T(8,128)(2,1)} %concatenate.17, s32[30720]{0:T(1024)S(1)} %get-tuple-element.57), kind=kCustom, calls=%fused_computation.2 | custom fusion | bytes 125952000 | tf_op jit(solution)/shard_map/gather | solution.py:64
  671.6 12.9 all-to-all-start.2
  684.6 24.3 fusion.41
  710.4 7.8 concatenate.16
  718.2 154.2 %gather_fusion.1 = bf16[30720,1024]{1,0:T(8,128)(2,1)} fusion(bf16[4097,1024]{1,0:T(8,128)(2,1)} %concatenate.16, s32[30720]{0:T(1024)S(1)} %get-tuple-element.57), kind=kCustom, calls=%fused_computation.1 | custom fusion | bytes 125952000 | tf_op jit(solution)/shard_map/gather | solution.py:65
  872.4 489.2 %all-to-all-done.2 = bf16[4,16,480,1024]{3,2,1,0:T(8,128)(2,1)} async-done(((bf16[4,16,480,1024]{3,2,1,0:T(8,128)(2,1)}), bf16[4,16,480,1024]{3,2,1,0:T(8,128)(2,1)}, u32[]{:S(2)}, u32[]{:S(2)}) %all-to-all-start.2) | async-done | bytes 62914592 | tf_op jit(solution)/shard_map/all_to_all | solution.py:67
  1361.6 12.8 all-to-all-start.1
  1376.4 71.8 %fusion.12 = f32[16,4,480,704]{2,3,1,0:T(8,128)} fusion(bf16[4,16,480,1024]{3,2,1,0:T(8,128)(2,1)} %all-to-all-done.2, bf16[16,1024,704]{1,2,0:T(8,128)(2,1)} %all-gather.11.cloned.1.call-done), kind=kOutput, calls=%fused_computation.27 | convolution fusion | flops 44291850240 | bytes 172490752 | tf_op jit(solution)/shard_map/secd,edf->secf/dot_general | solution.py:32
  1448.2 742.3 %all-to-all-done.1 = bf16[4,16,480,1024]{3,2,1,0:T(8,128)(2,1)} async-done(((bf16[4,16,480,1024]{3,2,1,0:T(8,128)(2,1)}), bf16[4,16,480,1024]{3,2,1,0:T(8,128)(2,1)}, u32[]{:S(2)}, u32[]{:S(2)}) %all-to-all-start.1) | async-done | bytes 62914592 | tf_op jit(solution)/shard_map/all_to_all | solution.py:68
  2190.5 71.8 %fusion.18 = f32[16,4,480,704]{2,3,1,0:T(8,128)} fusion(f32[4,16,480]{2,0,1:T(4,128)S(1)} %copy.81, bf16[4,16,480,1024]{3,2,1,0:T(8,128)(2,1)} %all-to-all-done.1, bf16[16,704,1024]{2,1,0:T(8,128)(2,1)} %all-gather.7.cloned.1.call-done), kind=kOutput, calls=%fused_computation.32 | convolution fusion | flops 44386222080 | bytes 172613632 | tf_op jit(solution)/shard_map/secd,efd->secf/dot_general | solution.py:37
  2262.3 158.2 %fusion.9 = (bf16[4,16,480,704]{2,3,0,1:T(8,128)(2,1)}, bf16[4,16,480,704]{2,3,0,1:T(8,128)(2,1)}, bf16[4,16,480,704]{2,3,0,1:T(8,128)(2,1)}) fusion(f32[16,4,480,704]{2,3,1,0:T(8,128)} %fusion.12, f32[16,4,480,704]{2,3,1,0:T(8,128)} %fusion.18, bf16[16,1024,704]{1,2,0:T(8,128)(2,1)} %all-gather.9.cloned.1.call-done, ...), kind=kOutput, calls=%fused_computation.23 | convolution fusion | flops 44616253440 | bytes 388759552 | tf_op jit(solution)/shard_map/secd,edf->secf/dot_general | solution.py:33
  2420.5 59.9 %fusion.38 = f32[16,704,1024]{2,1,0:T(8,128)} fusion(bf16[4,16,480,704]{2,3,0,1:T(8,128)(2,1)} %get-tuple-element.51, f32[4,16,480]{2,0,1:T(4,128)S(1)} %copy-done.7, bf16[4,16,480,1024]{3,2,1,0:T(8,128)(2,1)} %all-to-all-done.1), kind=kOutput, calls=%fused_computation.53 | convolution fusion | flops 44386222080 | bytes 152428544 | tf_op jit(solution)/shard_map/secf,secd->efd/dot_general | solution.py:42
  2480.5 59.7 %fusion.35 = f32[16,1024,704]{1,2,0:T(8,128)} fusion(bf16[4,16,480,1024]{3,2,1,0:T(8,128)(2,1)} %all-to-all-done.2, bf16[4,16,480,704]{2,3,0,1:T(8,128)(2,1)} %get-tuple-element.53), kind=kOutput, calls=%fused_computation.52 | convolution fusion | flops 44291850240 | bytes 152305664 | tf_op jit(solution)/shard_map/secd,secf->edf/dot_general | solution.py:43
  2540.3 59.7 %fusion.32 = f32[16,1024,704]{1,2,0:T(8,128)} fusion(bf16[4,16,480,1024]{3,2,1,0:T(8,128)(2,1)} %all-to-all-done.2, bf16[4,16,480,704]{2,3,0,1:T(8,128)(2,1)} %get-tuple-element.52), kind=kOutput, calls=%fused_computation.51 | convolution fusion | flops 44291850240 | bytes 152305664 | tf_op jit(solution)/shard_map/secd,secf->edf/dot_general | solution.py:41
  2600.0 68.8 %fusion.1 = f32[4,16,480]{2,0,1:T(4,128)S(1)} fusion(bf16[4,16,480,1024]{3,2,1,0:T(8,128)(2,1)} %all-to-all-done.1, bf16[4,16,480,704]{2,3,0,1:T(8,128)(2,1)} %get-tuple-element.51, bf16[16,704,1024]{2,1,0:T(8,128)(2,1)} %all-gather.7.cloned.1.call-done), kind=kOutput, calls=%fused_computation.9 | convolution fusion | flops 44386189312 | bytes 129359872 | tf_op jit(solution)/shard_map/secf,efd->secd/dot_general | solution.py:79
  2669.5 4.2 all-to-all-start.4
  2673.7 71.7 %fusion.24 = f32[16,4,480,1024]{3,2,1,0:T(8,128)} fusion(bf16[4,16,480,704]{2,3,0,1:T(8,128)(2,1)} %get-tuple-element.52, bf16[16,1024,704]{1,2,0:T(8,128)(2,1)} %all-gather.11.cloned.1.call-done), kind=kOutput, calls=%fused_computation.37 | convolution fusion | flops 44291850240 | bytes 192151552 | tf_op jit(solution)/shard_map/secf,edf->secd/dot_general | solution.py:40
  2745.4 90.9 %fusion.11 = bf16[4,16,480,1024]{3,2,0,1:T(8,128)(2,1)} fusion(f32[16,4,480,1024]{3,2,1,0:T(8,128)} %fusion.24, bf16[4,16,480,704]{2,3,0,1:T(8,128)(2,1)} %get-tuple-element.53, bf16[16,1024,704]{1,2,0:T(8,128)(2,1)} %all-gather.9.cloned.1.call-done), kind=kOutput, calls=%fused_computation.26 | convolution fusion | flops 44354764800 | bytes 255066112 | tf_op jit(solution)/shard_map/secf,edf->secd/dot_general | solution.py:40
  2836.3 41.5 copy.85
  2877.8 13.1 all-to-all-start.3
  2891.0 19.1 fusion.56
  2910.2 3.4 copy.90
  2913.5 3.4 copy.91
  2918.0 135.5 %gather_fusion.4 = f32[24576]{0:T(1024)S(1)} fusion(f32[30721]{0:T(1024)S(1)} %pad_maximum_fusion, s32[24576]{0:T(1024)S(1)} %broadcast_clamp_fusion), kind=kCustom, calls=%fused_computation.4 | custom fusion | bytes 294912 | tf_op jit(solution)/shard_map/gather | solution.py:84
  3053.5 2.1 reshape.117
  3056.9 511.1 %all-to-all-done.3 = bf16[4,16,480,1024]{3,2,1,0:T(8,128)(2,1)} async-done(((bf16[4,16,480,1024]{3,2,1,0:T(8,128)(2,1)}), bf16[4,16,480,1024]{3,2,1,0:T(8,128)(2,1)}, u32[]{:S(2)}, u32[]{:S(2)}) %all-to-all-start.3) | async-done | bytes 62914592 | tf_op jit(solution)/shard_map/all_to_all | solution.py:81
  3568.0 41.0 concatenate.18
  3609.1 449.3 %gather_fusion.3 = bf16[24576,1024]{1,0:T(8,128)(2,1)} fusion(bf16[30721,1024]{1,0:T(8,128)(2,1)} %concatenate.18, s32[24576]{0:T(1024)S(1)} %broadcast_clamp_fusion), kind=kCustom, calls=%fused_computation.3 | custom fusion | bytes 100761600 | tf_op jit(solution)/shard_map/gather | solution.py:83
  4058.3 84.5 %reshape.118 = f32[4096,6,1024]{2,1,0:T(8,128)} reshape(bf16[24576,1024]{1,0:T(8,128)(2,1)} %gather_fusion.3) | data formatting | bytes 150994944 | tf_op jit(solution)/shard_map/convert_element_type | solution.py:86
  4142.8 48.3 %reduce_sum.28 = f32[4096,1024]{1,0:T(8,128)} reduce(f32[4096,6,1024]{2,1,0:T(8,128)} %reshape.118, f32[]{:T(128)} %constant.40.clone.1), dimensions={1}, to_apply=%region_5.6 | reduce | flops 20971520 | bytes 117440512 | tf_op jit(solution)/shard_map/reduce_sum | solution.py:86
  4191.1 24.8 add_convert_fusion.1
  (83 shorter events, 20.8 us)
Async XLA Ops:
  7.2 44.3 %all-gather.15.cloned.1.call-start = ((), (), s32[]{:S(2)}) async-start(), calls=%async_computation.15 | async-start | bytes 4325376 | tf_op jit(solution)/shard_map/all_gather | solution.py:74
  7.9 84.3 %all-gather.17.cloned.1.call-start = ((), (), s32[]{:S(2)}) async-start(), calls=%async_computation.16 | async-start | bytes 4325376 | tf_op jit(solution)/shard_map/all_gather | solution.py:73
  8.6 124.3 %all-gather.13.cloned.1.call-start = ((), (), s32[]{:S(2)}) async-start(), calls=%async_computation.14 | async-start | bytes 4325376 | tf_op jit(solution)/shard_map/all_gather | solution.py:75
  9.4 1366.9 %reduce-scatter.13.cloned.1.call-start = ((), (), s32[]{:S(2)}) async-start(), calls=%async_computation.20 | async-start | bytes 8650752 | tf_op jit(solution)/shard_map/reduce_scatter | solution.py:90
  166.9 19.7 copy-start.2
  186.5 1189.7 %reduce-scatter.17.cloned.1.call-start = ((), (), s32[]{:S(2)}) async-start(), calls=%async_computation.22 | async-start | bytes 8650752 | tf_op jit(solution)/shard_map/reduce_scatter | solution.py:92
  191.9 3.4 copy-start
  222.8 20.1 copy-start.5
  242.9 262.0 %copy-start.3 = (s32[24576,1]{0,1:T(1,128)}, s32[24576,1]{0,1:T(1,128)S(1)}, u32[]{:S(2)}) copy-start(s32[24576,1]{0,1:T(1,128)S(1)} %compare_select_fusion) | copy-start | bytes 294916
  505.7 166.0 %all-to-all-start = ((f32[4,16,480]{2,1,0:T(8,128)}), f32[4,16,480]{2,1,0:T(8,128)}, u32[]{:S(2)}, u32[]{:S(2)}) async-start(f32[4,16,480]{2,1,0:T(8,128)} %reshape.112), calls=%async_computation | async-start | bytes 262144 | tf_op jit(solution)/shard_map/all_to_all | solution.py:69
  671.6 690.0 %all-to-all-start.2 = ((bf16[4,16,480,1024]{3,2,1,0:T(8,128)(2,1)}), bf16[4,16,480,1024]{3,2,1,0:T(8,128)(2,1)}, u32[]{:S(2)}, u32[]{:S(2)}) async-start(bf16[4,16,480,1024]{3,2,1,0:T(8,128)(2,1)} %bitcast.132), calls=%async_computation.2 | async-start | bytes 125829120 | tf_op jit(solution)/shard_map/all_to_all | solution.py:67
  684.6 691.7 %reduce-scatter.15.cloned.1.call-start = ((), (), s32[]{:S(2)}) async-start(), calls=%async_computation.21 | async-start | bytes 8650752 | tf_op jit(solution)/shard_map/reduce_scatter | solution.py:91
  708.9 667.5 %all-gather.11.cloned.1.call-start = ((), (), s32[]{:S(2)}) async-start(), calls=%async_computation.13 | async-start | bytes 34603008 | tf_op jit(solution)/shard_map/all_gather | solution.py:70
  709.7 738.6 %all-gather.7.cloned.1.call-start = ((), (), s32[]{:S(2)}) async-start(), calls=%async_computation.11 | async-start | bytes 34603008 | tf_op jit(solution)/shard_map/all_gather | solution.py:72
  1361.6 828.9 %all-to-all-start.1 = ((bf16[4,16,480,1024]{3,2,1,0:T(8,128)(2,1)}), bf16[4,16,480,1024]{3,2,1,0:T(8,128)(2,1)}, u32[]{:S(2)}, u32[]{:S(2)}) async-start(bf16[4,16,480,1024]{3,2,1,0:T(8,128)(2,1)} %bitcast.131), calls=%async_computation.1 | async-start | bytes 125829120 | tf_op jit(solution)/shard_map/all_to_all | solution.py:68
  1374.4 887.9 %all-gather.9.cloned.1.call-start = ((), (), s32[]{:S(2)}) async-start(), calls=%async_computation.12 | async-start | bytes 34603008 | tf_op jit(solution)/shard_map/all_gather | solution.py:71
  1375.2 1535.0 %all-reduce.8.cloned.1.call-start = ((), (), s32[]{:S(2)}) async-start(), calls=%async_computation.23 | async-start | bytes 17301504 | tf_op jit(solution)/shard_map/psum | solution.py:90
  1376.2 814.3 %copy-start.6 = (f32[4,16,480]{2,0,1:T(4,128)}, f32[4,16,480]{2,0,1:T(4,128)S(1)}, u32[]{:S(2)}) copy-start(f32[4,16,480]{2,0,1:T(4,128)S(1)} %copy.81) | copy-start | bytes 368644
  1376.3 2839.6 %reduce-scatter.9.cloned.1.call-start = ((), (), s32[]{:S(2)}) async-start(), calls=%async_computation.18 | async-start | bytes 69206016 | tf_op jit(solution)/shard_map/reduce_scatter | solution.py:89
  2262.3 158.2 %copy-start.7 = (f32[4,16,480]{2,0,1:T(4,128)S(1)}, f32[4,16,480]{2,0,1:T(4,128)}, u32[]{:S(2)}) copy-start(f32[4,16,480]{2,0,1:T(4,128)} %copy-done.6) | copy-start | bytes 368644
  2480.5 1735.5 %reduce-scatter.11.cloned.1.call-start = ((), (), s32[]{:S(2)}) async-start(), calls=%async_computation.19 | async-start | bytes 69206016 | tf_op jit(solution)/shard_map/reduce_scatter | solution.py:88
  2540.2 1675.7 %reduce-scatter.7.cloned.1.call-start = ((), (), s32[]{:S(2)}) async-start(), calls=%async_computation.17 | async-start | bytes 69206016 | tf_op jit(solution)/shard_map/reduce_scatter | solution.py:87
  2669.5 208.3 %all-to-all-start.4 = ((f32[4,16,480]{2,1,0:T(8,128)}), f32[4,16,480]{2,1,0:T(8,128)}, u32[]{:S(2)}, u32[]{:S(2)}) async-start(f32[4,16,480]{2,1,0:T(8,128)} %copy.86), calls=%async_computation.4 | async-start | bytes 262144 | tf_op jit(solution)/shard_map/all_to_all | solution.py:82
  2877.8 13.2 copy-start.4
  2877.8 690.2 %all-to-all-start.3 = ((bf16[4,16,480,1024]{3,2,1,0:T(8,128)(2,1)}), bf16[4,16,480,1024]{3,2,1,0:T(8,128)(2,1)}, u32[]{:S(2)}, u32[]{:S(2)}) async-start(bf16[4,16,480,1024]{3,2,1,0:T(8,128)(2,1)} %copy.85), calls=%async_computation.3 | async-start | bytes 125829120 | tf_op jit(solution)/shard_map/all_to_all | solution.py:81
  4191.1 24.8 copy-start.1
Sparse Core Ops, SparseCore 0:
  9.5 41.9 all-gather.14
  53.0 39.1 all-gather.16
  93.7 39.1 all-gather.12
  186.7 68.5 reduce-scatter.12
  257.4 68.5 reduce-scatter.16
  709.0 69.0 reduce-scatter.14
  779.7 267.9 all-gather.10
  1049.2 267.9 all-gather.6
  1376.8 268.4 all-gather.8
  1647.8 291.2 all-reduce.7
  2480.6 500.0 reduce-scatter.8
  2983.3 501.1 reduce-scatter.10
  3487.4 501.1 reduce-scatter.6
where the time goes:
time: 4240 us; the launch traced here: 4220 us
  waiting for transfers between devices  1830 us (43%)
  local copies, waits for them, and re-layouts  1370 us (32%)
  matrix products  893 us (21%)
  other arithmetic  66.2 us (2%)
  starting transfers between devices  47.5 us (1%)
    all_to_all x1, waiting for transfers between devices, device_step(): dy_recv = lax.all_to_all(dy_send, 'ep', 0, 0, tiled=True)  742 us
    all_to_all x1, waiting for transfers between devices, device_step(): lax.all_to_all(dx_recv, 'ep', 0, 0, tiled=True)  511 us
    all_to_all x1, waiting for transfers between devices, device_step(): x_recv = lax.all_to_all(x_send, 'ep', 0, 0, tiled=True)  489 us
    gather x1, local copies, waits for them, and re-layouts, device_step(): jnp.concatenate([dx_back, zero_row])[slot_idx]  449 us
    dot_general x2, matrix products, swiglu_backward(): jnp.einsum(up_form, x_rows, w_c, preferred_element_type=jnp.float32)  178 us
    gather x1, local copies, waits for them, and re-layouts, device_step(): jnp.concatenate([gate_loc.reshape(-1), zero_one])[filled]  169 us
    gather x1, local copies, waits for them, and re-layouts, device_step(): x_send = jnp.concatenate([x_loc, zero_row])[tok_src].reshape(buf_shape)  154 us
    gather x1, local copies, waits for them, and re-layouts, device_step(): dy_send = jnp.concatenate([dy_loc, zero_row])[tok_src].reshape(buf_shape)  154 us
  transfers between devices with their start and end apart: 18, of which 6 were waited for; matrix products, arithmetic and copies ran while one was open for 54% of the time, Pallas kernels for 0%

commit v1 on v0

v1 whole, which is shorter than its diff:
```python
import jax
import jax.numpy as jnp
from jax import lax
from jax.experimental import pallas as pl
from jax.experimental.pallas import tpu as pltpu
from jax.sharding import PartitionSpec as P

CAP_NUM = 5
CAP_DEN = 4
LANES = 128
UNROLL = 8
CHUNKS = 4


def capacity_for(tok_dev, top_k, n_exp):
    needed = -(-(tok_dev * top_k * CAP_NUM) // (CAP_DEN * n_exp))
    return max(8, -(-needed // 8) * 8)


def route_slots(ids_dev, gate_dev, n_exp, capacity):
    top_k = ids_dev.shape[1]
    flat_ids = ids_dev.reshape(-1)
    n_assign = flat_ids.shape[0]
    onehot = (flat_ids[:, None] == jnp.arange(n_exp, dtype=jnp.int32)[None, :]).astype(jnp.int32)
    slot_pos = jnp.sum(jnp.cumsum(onehot, axis=0) * onehot, axis=1) - 1
    slot_idx = jnp.where(slot_pos < capacity, flat_ids * capacity + slot_pos, n_exp * capacity)
    tokens = jnp.zeros((n_exp * capacity + 1,), jnp.int32).at[slot_idx].set(jnp.arange(n_assign, dtype=jnp.int32) // top_k)
    gates = jnp.zeros((n_exp * capacity + 1,), jnp.float32).at[slot_idx].set(gate_dev.reshape(-1))
    return slot_idx, tokens[: n_exp * capacity], gates[: n_exp * capacity]


def gather_rows(tables, tokens, n_local, capacity):
    n_src = len(tables)
    tok_dev, dim = tables[0].shape
    parts = dim // LANES

    def body(tok_ref, *refs):
        tabs, out_ref, raw, wide, rows, sem = refs[:n_src], *refs[n_src:]
        src = pl.program_id(0)
        expert = pl.program_id(1)

        @pl.when(expert == 0)
        def _():
            for m in range(n_src):
                @pl.when(src == m)
                def _():
                    copy = pltpu.make_async_copy(tabs[m], raw, sem)
                    copy.start()
                    copy.wait()

            @pl.loop(0, tok_dev // LANES)
            def _(i):
                base = pl.multiple_of(i * LANES, LANES)
                for j in range(parts):
                    piece = raw[pl.ds(base, LANES), j * LANES : (j + 1) * LANES].astype(jnp.float32)
                    wide[pl.ds(base * parts + j, LANES, stride=parts), :] = piece

        first = expert * capacity

        @pl.loop(0, capacity // UNROLL)
        def _(i):
            for k in range(UNROLL):
                slot = i * UNROLL + k
                tok = pl.multiple_of(tok_ref[0, 0, first + slot] * parts, parts)
                rows[pl.ds(pl.multiple_of(slot * parts, parts), parts), :] = wide[pl.ds(tok, parts), :]

        for j in range(parts):
            out_ref[0, 0, :, j * LANES : (j + 1) * LANES] = rows[pl.ds(j, capacity, stride=parts), :].astype(out_ref.dtype)

    return pl.pallas_call(
        body,
        grid=(n_src, n_local),
        in_specs=[pl.BlockSpec((1, 1, n_local * capacity), lambda s, e: (s, 0, 0), memory_space=pltpu.SMEM)]
        + [pl.BlockSpec(memory_space=pl.ANY)] * n_src,
        out_specs=pl.BlockSpec((1, 1, capacity, dim), lambda s, e: (e, s, 0, 0)),
        out_shape=jax.ShapeDtypeStruct((n_local, n_src, capacity, dim), tables[0].dtype),
        scratch_shapes=[
            pltpu.VMEM((tok_dev, dim), tables[0].dtype),
            pltpu.VMEM((tok_dev * parts, LANES), jnp.float32),
            pltpu.VMEM((capacity * parts, LANES), jnp.float32),
            pltpu.SemaphoreType.DMA,
        ],
        compiler_params=pltpu.CompilerParams(vmem_limit_bytes=40 * 2**20),
        cost_estimate=pl.CostEstimate(flops=600_000_000, bytes_accessed=100_000_000, transcendentals=0),
        name="gather_rows",
    )(tokens.reshape(n_src, 1, n_local * capacity), *tables)


def sum_rows(row_chunks, tokens, tok_dev):
    n_chunks = len(row_chunks)
    per_chunk, n_src, capacity, dim = row_chunks[0].shape
    n_local = per_chunk * n_chunks
    parts = dim // LANES

    def body(tok_ref, *refs):
        chunks, out_ref, wide = refs[:n_chunks], *refs[n_chunks:]
        step = pl.program_id(1)

        @pl.when(step == 0)
        def _():
            @pl.loop(0, tok_dev * parts // 256)
            def _(i):
                out_ref[0, pl.ds(pl.multiple_of(i * 256, 256), 256), :] = jnp.zeros((256, LANES), jnp.float32)

        for c in range(n_chunks):
            for j in range(parts):
                wide[pl.ds(j, capacity, stride=parts), :] = chunks[c][0, 0, :, j * LANES : (j + 1) * LANES].astype(jnp.float32)
            first = (step + c * per_chunk) * capacity

            @pl.loop(0, capacity // UNROLL)
            def _(i):
                where, sums = [], []
                for k in range(UNROLL):
                    slot = i * UNROLL + k
                    tok = pl.multiple_of(tok_ref[0, 0, first + slot] * parts, parts)
                    where.append(tok)
                    row = wide[pl.ds(pl.multiple_of(slot * parts, parts), parts), :]
                    sums.append(out_ref[0, pl.ds(tok, parts), :] + row)
                for k in reversed(range(UNROLL)):
                    out_ref[0, pl.ds(where[k], parts), :] = sums[k]

    return pl.pallas_call(
        body,
        grid=(n_src, per_chunk),
        in_specs=[pl.BlockSpec((1, 1, n_local * capacity), lambda s, e: (s, 0, 0), memory_space=pltpu.SMEM)]
        + [pl.BlockSpec((1, 1, capacity, dim), lambda s, e: (e, s, 0, 0))] * n_chunks,
        out_specs=pl.BlockSpec((1, tok_dev * parts, LANES), lambda s, e: (s, 0, 0)),
        out_shape=jax.ShapeDtypeStruct((n_src, tok_dev * parts, LANES), jnp.float32),
        scratch_shapes=[pltpu.VMEM((capacity * parts, LANES), jnp.float32)],
        compiler_params=pltpu.CompilerParams(vmem_limit_bytes=56 * 2**20),
        cost_estimate=pl.CostEstimate(flops=600_000_000, bytes_accessed=130_000_000, transcendentals=0),
        name="sum_rows",
    )(tokens.reshape(n_src, 1, n_local * capacity), *row_chunks)


def swiglu_hidden(h_one, h_three, d_act):
    sig_one = jax.nn.sigmoid(h_one)
    silu_one = h_one * sig_one
    return silu_one * h_three, d_act * h_three * sig_one * (1.0 + h_one * (1.0 - sig_one)), d_act * silu_one


def dot32(form, a, b):
    return jnp.einsum(form, a, b, preferred_element_type=jnp.float32)


def solution(mesh):
    ep_size = mesh.shape["ep"]
    fs_size = mesh.shape["fsdp"]
    tok_spec = P(("fsdp", "ep"), None)
    in_specs = (tok_spec, tok_spec, tok_spec, tok_spec, P("ep", "fsdp", None), P("ep", None, "fsdp"), P("ep", "fsdp", None), P("fsdp", None), P(None, "fsdp"), P("fsdp", None))
    out_specs = (tok_spec, tok_spec, P("ep", "fsdp", None), P("ep", None, "fsdp"), P("ep", "fsdp", None), P("fsdp", None), P(None, "fsdp"), P("fsdp", None))

    def swap(value, bit):
        return lax.ppermute(value, "ep", [(i, i ^ bit) for i in range(ep_size)])

    def swap_fs(value):
        return lax.ppermute(value, "fsdp", [(i, i ^ 1) for i in range(fs_size)])

    def device_step(x_loc, dy_loc, ids_loc, gate_loc, w_one, w_two, w_three, ws_one, ws_two, ws_three):
        tok_dev, top_k = ids_loc.shape
        model_dim = x_loc.shape[1]
        n_local, _, ff = w_one.shape
        n_exp = n_local * ep_size
        capacity = capacity_for(tok_dev, top_k, n_exp)
        me = lax.axis_index("ep")
        row = lax.axis_index("fsdp")
        pick = lambda a, i, axis=0: lax.dynamic_index_in_dim(a, i, axis, keepdims=False)

        def spread(value):
            across = swap(value, 2)
            return [value, swap(value, 1), across, swap(across, 1)]

        x_tabs = spread(x_loc)
        dy_tabs = spread(dy_loc)

        slot_idx, slot_tok, slot_gate = route_slots(ids_loc, gate_loc, n_exp, capacity)
        table = jnp.stack([slot_tok.astype(jnp.float32), slot_gate]).reshape(2, ep_size, n_local, capacity).swapaxes(0, 1)
        table = lax.all_to_all(table, "ep", 0, 0, tiled=True)
        table = jnp.stack([pick(table, me ^ m) for m in range(ep_size)])
        tokens = table[:, 0].astype(jnp.int32)
        gates = table[:, 1].swapaxes(0, 1).reshape(n_local, ep_size * capacity, 1)

        per = n_local // CHUNKS
        weights = []
        for c in range(CHUNKS):
            part = slice(c * per, (c + 1) * per)
            weights.append((
                lax.all_gather(w_one[part], "fsdp", axis=1, tiled=True),
                lax.all_gather(w_three[part], "fsdp", axis=1, tiled=True),
                lax.all_gather(w_two[part], "fsdp", axis=2, tiled=True),
            ))
        ws_one_full = lax.all_gather(ws_one, "fsdp", axis=0, tiled=True)
        ws_three_full = lax.all_gather(ws_three, "fsdp", axis=0, tiled=True)
        ws_two_full = lax.all_gather(ws_two, "fsdp", axis=1, tiled=True)

        x_rows = gather_rows(x_tabs, tokens, n_local, capacity).reshape(n_local, ep_size * capacity, model_dim)
        dy_rows = gather_rows(dy_tabs, tokens, n_local, capacity).reshape(n_local, ep_size * capacity, model_dim)

        dx_chunks, dgate_chunks, grads = [], [], []
        for c in range(CHUNKS):
            part = slice(c * per, (c + 1) * per)
            w_a, w_c, w_b = weights[c]
            x_c, gate_c = x_rows[part], gates[part]
            dy_c = dy_rows[part].astype(jnp.float32)
            g_c = (gate_c * dy_c).astype(jnp.bfloat16)
            h_one = dot32("erd,edf->erf", x_c, w_a)
            h_three = dot32("erd,edf->erf", x_c, w_c)
            d_act = dot32("erd,efd->erf", g_c, w_b)
            kept = gate_c > 0
            act, dh_one, dh_three = [jnp.where(kept, v, 0.0).astype(jnp.bfloat16) for v in swiglu_hidden(h_one, h_three, d_act)]
            dw_two = dot32("erf,erd->efd", act, g_c)
            dw_one = dot32("erd,erf->edf", x_c, dh_one)
            dw_three = dot32("erd,erf->edf", x_c, dh_three)
            grads.append((
                lax.psum_scatter(dw_one, "fsdp", scatter_dimension=1, tiled=True),
                lax.psum_scatter(dw_two, "fsdp", scatter_dimension=2, tiled=True),
                lax.psum_scatter(dw_three, "fsdp", scatter_dimension=1, tiled=True),
            ))
            dx_c = (dot32("erf,edf->erd", dh_one, w_a) + dot32("erf,edf->erd", dh_three, w_c)).astype(jnp.bfloat16)
            dx_chunks.append(dx_c.reshape(per, ep_size, capacity, model_dim))
            y_c = dot32("erf,efd->erd", act, w_b)
            dgate_chunks.append(jnp.sum(dy_c * y_c, axis=-1))

        dx_part = sum_rows(dx_chunks, tokens, tok_dev)
        from_core = swap(dx_part[3], 1)
        to_chip = dx_part[2] + from_core
        from_chip = swap(to_chip, 2)
        dx_near = swap(dx_part[1], 1)

        dgate = jnp.concatenate(dgate_chunks).reshape(n_local, ep_size, capacity).swapaxes(0, 1)
        dgate = jnp.stack([pick(dgate, me ^ k) for k in range(ep_size)])
        dgate = lax.all_to_all(dgate, "ep", 0, 0, tiled=True).reshape(-1)
        dgate_loc = jnp.concatenate([dgate, jnp.zeros((1,), jnp.float32)])[slot_idx].reshape(tok_dev, top_k)

        h_one = dot32("td,df->tf", x_loc, ws_one_full)
        h_three = dot32("td,df->tf", x_loc, ws_three_full)
        d_act = dot32("td,fd->tf", dy_loc, ws_two_full)
        act, dh_one, dh_three = [v.astype(jnp.bfloat16) for v in swiglu_hidden(h_one, h_three, d_act)]
        sff = act.shape[1]
        dx_shared = (dot32("tf,df->td", dh_one, ws_one_full) + dot32("tf,df->td", dh_three, ws_three_full)).astype(jnp.bfloat16)
        shared = jnp.stack([dot32("td,tf->df", x_loc, dh_one), dot32("td,tf->df", dy_loc, act), dot32("td,tf->df", x_loc, dh_three)])
        shared = shared.reshape(3, fs_size, ep_size, model_dim // (fs_size * ep_size), sff)
        by_place = [pick(shared, me ^ m, 2) for m in range(ep_size)]
        near = by_place[0] + swap(by_place[1], 1)
        far = by_place[2] + swap(by_place[3], 1)
        near = near + swap(far, 2)
        mine = pick(near, row, 1) + swap_fs(pick(near, row ^ 1, 1))
        pieces = jnp.stack(spread(mine), axis=1)
        pieces = jnp.stack([pick(pieces, me ^ k, 1) for k in range(ep_size)], axis=1).reshape(3, model_dim // fs_size, sff)

        total = (dx_part[0] + dx_near) + from_chip
        dx_loc = (total.reshape(tok_dev, model_dim) + dx_shared.astype(jnp.float32)).astype(jnp.bfloat16)
        dw_one, dw_two, dw_three = [jnp.concatenate([g[i] for g in grads]) for i in range(3)]
        return dx_loc, dgate_loc, dw_one, dw_two, dw_three, pieces[0], pieces[1].T, pieces[2]

    return jax.shard_map(device_step, mesh=mesh, in_specs=in_specs, out_specs=out_specs, check_vma=False)
```

time: 4240 us -> 3250 us (0.77)
  waiting for transfers between devices: 1830 us -> 821 us
  local copies, waits for them, and re-layouts: 1370 us -> 650 us
  Pallas kernels: 0 us -> 358 us
  other arithmetic: 66.2 us -> 326 us
  matrix products: 893 us -> 1050 us
    all_to_all x5 -> x2, waiting for transfers between devices: 1740 us -> 278 us  [the longest x1 272 us: device_step(): dgate = lax.all_to_all(dgate, 'ep', 0, 0, tiled=True).reshape(-1)]
    gather x5 -> x1, local copies, waits for them, and re-layouts: 1060 us -> 136 us  [device_step(): jnp.concatenate([dgate, jnp.zeros((1,), jnp.float32)])[slot_idx]]
    ppermute x0 -> x16, waiting for transfers between devices: none -> 537 us  [the longest x15 453 us: swap(): return lax.ppermute(value, 'ep', [(i, i ^ bit) for i in range(ep_size)])]
    pallas_call x0 -> x3, Pallas kernels: none -> 358 us  [the longest x2 240 us: gather_rows(): pl.pallas_call(body, grid=(n_src, n_local), in_specs=[pl.BlockSpec((1, 1,...]
    dot_general x17 -> x44, matrix products: 893 us -> 1050 us  [dot32(): return jnp.einsum(form, a, b, preferred_element_type=jnp.float32)]
    convert_element_type x0 -> x10, other arithmetic: none -> 126 us  [the longest x4 63.4 us: device_step(): dy_c = dy_rows[part].astype(jnp.float32)]
    slice x0 -> x16, local copies, waits for them, and re-layouts: none -> 108 us  [the longest x10 43.2 us: device_step(): x_c, gate_c = (x_rows[part], gates[part])]
    scatter x1 -> x2, local copies, waits for them, and re-layouts: 90.3 us -> 181 us  [the longest x1 90.3 us: route_slots(): jnp.zeros((n_exp * capacity + 1,), jnp.float32).at[slot_idx]]
  transfers between devices with their start and end apart: 18 -> 45, of which waited for: 6 -> 9; matrix products, arithmetic and copies ran while one was open for 54% -> 60% of each run, Pallas kernels for 0% -> 11%
where the time goes in v1:
time: 3250 us; the launch traced here: 3240 us
  matrix products  1050 us (32%)
  waiting for transfers between devices  821 us (25%)
  local copies, waits for them, and re-layouts  650 us (20%)
  Pallas kernels  358 us (11%)
  other arithmetic  326 us (10%)
    dot_general x44, matrix products, dot32(): return jnp.einsum(form, a, b, preferred_element_type=jnp.float32)  1050 us
    ppermute x15, waiting for transfers between devices, swap(): return lax.ppermute(value, 'ep', [(i, i ^ bit) for i in range(ep_size)])  453 us
    all_to_all x1, waiting for transfers between devices, device_step(): dgate = lax.all_to_all(dgate, 'ep', 0, 0, tiled=True).reshape(-1)  272 us
    pallas_call x2, Pallas kernels, gather_rows(): pl.pallas_call(body, grid=(n_src, n_local), in_specs=[pl.BlockSpec((1, 1,...  240 us
    gather x1, local copies, waits for them, and re-layouts, device_step(): jnp.concatenate([dgate, jnp.zeros((1,), jnp.float32)])[slot_idx]  136 us
    convert_element_type x4, local copies, waits for them, and re-layouts, device_step(): dy_c = dy_rows[part].astype(jnp.float32)  123 us
    pallas_call x1, Pallas kernels, sum_rows(): pl.pallas_call(body, grid=(n_src, per_chunk), in_specs=[pl.BlockSpec((1,...  117 us
    scatter x1, local copies, waits for them, and re-layouts, route_slots(): jnp.zeros((n_exp * capacity + 1,), jnp.float32).at[slot_idx]  90.3 us
  transfers between devices with their start and end apart: 45, of which 9 were waited for; matrix products, arithmetic and copies ran while one was open for 60% of the time, Pallas kernels for 11%

profile of v1, /device:TPU:0, one launch (start us, length us, event | category | flops | bytes accessed | tf_op | source)
XLA Modules:
  0.0 3240.3 jit_solution(14462708028804081342)
XLA Ops:
  76.5 146.9 %collective-permute-done.4.refs_2_ = bf16[4096,1024]{1,0:T(8,128)(2,1)} collective-permute-done((bf16[4096,1024]{1,0:T(8,128)(2,1)}, bf16[4096,1024]{1,0:T(8,128)(2,1)}, u32[]{:S(2)}, u32[]{:S(2)}) %collective-permute-start.4) | collective-permute-done | bytes 8388640 | tf_op jit(solution)/shard_map/ppermute | solution.py:154
  225.8 176.5 %collective-permute-done.1.refs_2_ = bf16[4096,1024]{1,0:T(8,128)(2,1)} collective-permute-done((bf16[4096,1024]{1,0:T(8,128)(2,1)}, bf16[4096,1024]{1,0:T(8,128)(2,1)}, u32[]{:S(2)}, u32[]{:S(2)}) %collective-permute-start.1) | collective-permute-done | bytes 8388640 | tf_op jit(solution)/shard_map/ppermute | solution.py:154
  404.8 90.3 %scatter_custom_fusion.1 = f32[30721]{0:T(1024)S(1)} fusion(s32[24576]{0:T(1024)S(1)} %bitcast.244, f32[24576]{0:T(1024)S(1)} %reshape.246, f32[]{:T(128)} %constant.87.clone.1), kind=kCustom, calls=%fused_computation.101 | custom fusion | bytes 122888 | tf_op jit(solution)/shard_map/scatter | solution.py:28
  495.2 90.3 %scatter_custom_fusion = s32[30721]{0:T(1024)S(1)} fusion(s32[24576]{0:T(1024)S(1)} %bitcast.245, s32[24576]{0:T(1024)S(1)} %add_select_fusion, s32[]{:T(128)} %constant.80.clone.1), kind=kCustom, calls=%fused_computation.103 | custom fusion | bytes 122888 | tf_op jit(solution)/shard_map/scatter | solution.py:27
  600.7 120.3 %gather_rows.3 = bf16[16,4,480,1024]{3,2,1,0:T(8,128)(2,1)} custom-call(s32[4,1,7680]{2,1,0:T(1,128)S(1)} %convert_element_type.135.tok_ref, bf16[4096,1024]{1,0:T(8,128)(2,1)S(1)} %copy-done, bf16[4096,1024]{1,0:T(8,128)(2,1)} %collective-permute-done.3.refs_1_, bf16[4096,1024]{1,0:T(8,128)(2,1)} %collective-permute-done.4.refs_2_, ...), custom_call_target="tpu_custom_call" | custom-call | flops 600000000 | bytes 100000000 | tf_op jit(solution)/shard_map/gather_rows/pallas_call | solution.py:70
  721.0 42.0 %fusion.25 = (bf16[4,4,480,1024]{3,2,1,0:T(8,128)(2,1)}, bf16[4,4,480,1024]{3,2,1,0:T(8,128)(2,1)}, bf16[4,4,480,1024]{3,2,1,0:T(8,128)(2,1)}, bf16[4,4,480,1024]{3,2,1,0:T(8,128)(2,1)}) fusion(bf16[16,4,480,1024]{3,2,1,0:T(8,128)(2,1)} %gather_rows.3), kind=kLoop, calls=%fused_computation.129 | loop fusion | bytes 125829120 | tf_op jit(solution)/shard_map/slice | solution.py:203
  763.1 120.1 %gather_rows.2 = bf16[16,4,480,1024]{3,2,1,0:T(8,128)(2,1)} custom-call(s32[4,1,7680]{2,1,0:T(1,128)S(1)} %convert_element_type.135.tok_ref, bf16[4096,1024]{1,0:T(8,128)(2,1)S(1)} %bitcast.211, bf16[4096,1024]{1,0:T(8,128)(2,1)} %collective-permute-done.refs_1_, bf16[4096,1024]{1,0:T(8,128)(2,1)} %collective-permute-done.1.refs_2_, ...), custom_call_target="tpu_custom_call" | custom-call | flops 600000000 | bytes 100000000 | tf_op jit(solution)/shard_map/gather_rows/pallas_call | solution.py:70
  883.1 36.6 %fusion.24 = (bf16[4,4,480,1024]{3,2,1,0:T(8,128)(2,1)S(1)}, bf16[4,4,480,1024]{3,2,1,0:T(8,128)(2,1)}, bf16[4,4,480,1024]{3,2,1,0:T(8,128)(2,1)}, bf16[4,4,480,1024]{3,2,1,0:T(8,128)(2,1)}) fusion(bf16[16,4,480,1024]{3,2,1,0:T(8,128)(2,1)} %gather_rows.2), kind=kLoop, calls=%fused_computation.128 | loop fusion | bytes 125829120 | tf_op jit(solution)/shard_map/slice | solution.py:204
  932.7 21.7 fusion.41
  954.3 21.7 fusion.40
  976.0 41.5 %select_convert_fusion = (bf16[4,1920,704]{1,2,0:T(8,128)(2,1)}, bf16[4,1920,704]{1,2,0:T(8,128)(2,1)}, bf16[4,1920,704]{1,2,0:T(8,128)(2,1)}) fusion(pred[4,1920]{1,0:T(4,128)(4,1)S(1)} %copy-done.16, f32[4,1920,704]{1,2,0:T(8,128)} %fusion.41, f32[4,1920,704]{1,2,0:T(8,128)} %fusion.40, bf16[4,1920,1024]{2,1,0:T(8,128)(2,1)} %bitcast.230, ...), kind=kOutput, calls=%fused_computation.23 | convolution fusion | flops 11170283520 | bytes 97197568 | tf_op jit(solution)/shard_map/erd,edf->erf/dot_general | solution.py:143
  1053.8 21.6 fusion.38
  1075.5 21.6 fusion.37
  1097.1 41.3 %select_convert_fusion.1 = (bf16[4,1920,704]{1,2,0:T(8,128)(2,1)}, bf16[4,1920,704]{1,2,0:T(8,128)(2,1)}, bf16[4,1920,704]{1,2,0:T(8,128)(2,1)}) fusion(pred[4,1920]{1,0:T(4,128)(4,1)S(1)} %broadcast_compare_fusion.1, f32[4,1920,704]{1,2,0:T(8,128)} %fusion.38, f32[4,1920,704]{1,2,0:T(8,128)} %fusion.37, bf16[4,1920,1024]{2,1,0:T(8,128)(2,1)} %bitcast.226, ...), kind=kOutput, calls=%fused_computation.24 | convolution fusion | flops 11170283520 | bytes 97197568 | tf_op jit(solution)/shard_map/erd,edf->erf/dot_general | solution.py:143
  1174.8 21.6 fusion.35
  1196.5 21.6 fusion.34
  1218.1 41.5 %select_convert_fusion.2 = (bf16[4,1920,704]{1,2,0:T(8,128)(2,1)}, bf16[4,1920,704]{1,2,0:T(8,128)(2,1)}, bf16[4,1920,704]{1,2,0:T(8,128)(2,1)}) fusion(pred[4,1920]{1,0:T(4,128)(4,1)S(1)} %broadcast_compare_fusion.2, f32[4,1920,704]{1,2,0:T(8,128)} %fusion.35, f32[4,1920,704]{1,2,0:T(8,128)} %fusion.34, bf16[4,1920,1024]{2,1,0:T(8,128)(2,1)} %bitcast.222, ...), kind=kOutput, calls=%fused_computation.25 | convolution fusion | flops 11170283520 | bytes 97197568 | tf_op jit(solution)/shard_map/erd,edf->erf/dot_general | solution.py:143
  1295.9 21.6 fusion.32
  1317.6 21.7 fusion.31
  1339.2 41.4 %select_convert_fusion.3 = (bf16[4,1920,704]{1,2,0:T(8,128)(2,1)}, bf16[4,1920,704]{1,2,0:T(8,128)(2,1)}, bf16[4,1920,704]{1,2,0:T(8,128)(2,1)}) fusion(pred[4,1920]{1,0:T(4,128)(4,1)S(1)} %broadcast_compare_fusion.3, f32[4,1920,704]{1,2,0:T(8,128)} %fusion.32, f32[4,1920,704]{1,2,0:T(8,128)} %fusion.31, bf16[4,1920,1024]{2,1,0:T(8,128)(2,1)} %bitcast.218, ...), kind=kOutput, calls=%fused_computation.26 | convolution fusion | flops 11170283520 | bytes 97197568 | tf_op jit(solution)/shard_map/erd,edf->erf/dot_general | solution.py:143
  1423.0 21.5 fusion.52
  1547.3 33.8 %multiply_convert_fusion.5 = (bf16[4096,1408]{1,0:T(8,128)(2,1)}, bf16[4096,1408]{1,0:T(8,128)(2,1)}) fusion(f32[4096,1408]{1,0:T(8,128)} %fusion.44, f32[4096,1408]{1,0:T(8,128)} %fusion.43, bf16[4096,1024]{1,0:T(8,128)(2,1)} %refs_0_.2, bf16[1408,1024]{1,0:T(8,128)(2,1)} %all-gather.40.cloned.1.call-done), kind=kOutput, calls=%fused_computation.19 | convolution fusion | flops 11886133248 | bytes 80478208 | tf_op jit(solution)/shard_map/td,fd->tf/dot_general | solution.py:143
  1600.6 25.4 fusion.8
  1690.3 91.9 %collective-permute-done.11 = f32[3,2,128,1408]{3,2,1,0:T(8,128)} collective-permute-done((f32[3,2,128,1408]{3,2,1,0:T(8,128)}, f32[3,2,128,1408]{3,2,1,0:T(8,128)}, u32[]{:S(2)}, u32[]{:S(2)}) %collective-permute-start.11) | collective-permute-done | bytes 4325408 | tf_op jit(solution)/shard_map/ppermute | solution.py:154
  1793.4 83.5 %collective-permute-done.12 = f32[3,128,1408]{2,1,0:T(8,128)S(1)} collective-permute-done((f32[3,128,1408]{2,1,0:T(8,128)}, f32[3,128,1408]{2,1,0:T(8,128)S(1)}, u32[]{:S(2)}, u32[]{:S(2)}) %collective-permute-start.12) | collective-permute-done | bytes 2162720 | tf_op jit(solution)/shard_map/ppermute | solution.py:157
  1900.8 27.8 collective-permute-done.14
  1949.8 21.3 fusion.33
  1992.3 22.2 fusion.39
  2014.5 22.3 fusion.42
  2036.8 25.1 add_convert_fusion.2
  2061.9 25.4 add_convert_fusion.1
  2087.4 25.6 add_convert_fusion
  2112.9 25.1 add_convert_fusion.3
  2138.1 117.3 %sum_rows.1 = f32[4,32768,128]{2,1,0:T(8,128)} custom-call(s32[4,1,7680]{2,1,0:T(1,128)} %copy-done.1, bf16[4,4,480,1024]{3,2,1,0:T(8,128)(2,1)} %bitcast.236, bf16[4,4,480,1024]{3,2,1,0:T(8,128)(2,1)} %bitcast.233, bf16[4,4,480,1024]{3,2,1,0:T(8,128)(2,1)} %bitcast.234, bf16[4,4,480,1024]{3,2,1,0:T(8,128)(2,1)} %bitcast.235), custom_call_target="tpu_custom_call" | custom-call | flops 600000000 | bytes 130000000 | tf_op jit(solution)/shard_map/sum_rows/pallas_call | solution.py:122
  2255.4 22.0 slice_bitcast_fusion.2
  2277.9 22.5 bitcast_convert_fusion
  2324.1 30.8 copy.82
  2354.9 30.8 copy.81
  2385.7 30.8 copy.80
  2434.2 30.8 copy.79
  2465.1 21.3 fusion.60
  2486.4 23.3 fusion.49
  2509.7 23.5 fusion.48
  2533.2 23.4 fusion.47
  2617.1 23.3 fusion.46
  2706.9 272.5 %all-to-all-done.1 = f32[4,16,480]{2,1,0:T(8,128)S(1)} async-done(((f32[4,16,480]{2,1,0:T(8,128)}), f32[4,16,480]{2,1,0:T(8,128)S(1)}, u32[]{:S(2)}, u32[]{:S(2)}) %all-to-all-start.1) | async-done | bytes 122912 | tf_op jit(solution)/shard_map/all_to_all | solution.py:232
  2979.6 135.5 %gather_fusion = f32[24576]{0:T(1024)S(1)} fusion(f32[30721]{0:T(1024)S(1)} %pad_maximum_fusion.8, s32[24576]{0:T(1024)S(1)} %copy-done.11), kind=kCustom, calls=%fused_computation | custom fusion | bytes 294912 | tf_op jit(solution)/shard_map/gather | solution.py:233
  3180.6 22.7 fusion.7
  (286 shorter events, 781.2 us)
Async XLA Ops:
  7.2 925.5 %all-gather.38.cloned.1.call-start = ((), (), s32[]{:S(2)}) async-start(), calls=%async_computation.25 | async-start | bytes 8650752 | tf_op jit(solution)/shard_map/all_gather | solution.py:188
  15.8 938.6 %all-gather.34.cloned.1.call-start = ((), (), s32[]{:S(2)}) async-start(), calls=%async_computation.23 | async-start | bytes 8650752 | tf_op jit(solution)/shard_map/all_gather | solution.py:190
  24.3 951.7 %all-gather.36.cloned.1.call-start = ((), (), s32[]{:S(2)}) async-start(), calls=%async_computation.24 | async-start | bytes 8650752 | tf_op jit(solution)/shard_map/all_gather | solution.py:189
  32.8 1021.0 %all-gather.32.cloned.1.call-start = ((), (), s32[]{:S(2)}) async-start(), calls=%async_computation.22 | async-start | bytes 8650752 | tf_op jit(solution)/shard_map/all_gather | solution.py:188
  33.4 1042.1 %all-gather.28.cloned.1.call-start = ((), (), s32[]{:S(2)}) async-start(), calls=%async_computation.20 | async-start | bytes 8650752 | tf_op jit(solution)/shard_map/all_gather | solution.py:190
  34.0 1063.1 %all-gather.30.cloned.1.call-start = ((), (), s32[]{:S(2)}) async-start(), calls=%async_computation.21 | async-start | bytes 8650752 | tf_op jit(solution)/shard_map/all_gather | solution.py:189
  34.5 1140.3 %all-gather.26.cloned.1.call-start = ((), (), s32[]{:S(2)}) async-start(), calls=%async_computation.19 | async-start | bytes 8650752 | tf_op jit(solution)/shard_map/all_gather | solution.py:188
  35.3 1161.2 %all-gather.22.cloned.1.call-start = ((), (), s32[]{:S(2)}) async-start(), calls=%async_computation.17 | async-start | bytes 8650752 | tf_op jit(solution)/shard_map/all_gather | solution.py:190
  36.0 1182.1 %all-gather.24.cloned.1.call-start = ((), (), s32[]{:S(2)}) async-start(), calls=%async_computation.18 | async-start | bytes 8650752 | tf_op jit(solution)/shard_map/all_gather | solution.py:189
  36.8 1259.2 %all-gather.20.cloned.1.call-start = ((), (), s32[]{:S(2)}) async-start(), calls=%async_computation.16 | async-start | bytes 8650752 | tf_op jit(solution)/shard_map/all_gather | solution.py:188
  37.4 1280.2 %all-gather.16.cloned.1.call-start = ((), (), s32[]{:S(2)}) async-start(), calls=%async_computation.14 | async-start | bytes 8650752 | tf_op jit(solution)/shard_map/all_gather | solution.py:190
  38.1 1301.1 %all-gather.18.cloned.1.call-start = ((), (), s32[]{:S(2)}) async-start(), calls=%async_computation.15 | async-start | bytes 8650752 | tf_op jit(solution)/shard_map/all_gather | solution.py:189
  38.7 1448.3 %all-gather.44.cloned.1.call-start = ((), (), s32[]{:S(2)}) async-start(), calls=%async_computation.28 | async-start | bytes 4325376 | tf_op jit(solution)/shard_map/all_gather | solution.py:192
  38.7 184.7 %collective-permute-start.4 = (bf16[4096,1024]{1,0:T(8,128)(2,1)}, bf16[4096,1024]{1,0:T(8,128)(2,1)}, u32[]{:S(2)}, u32[]{:S(2)}) collective-permute-start(bf16[4096,1024]{1,0:T(8,128)(2,1)} %refs_0_.3), channel_id=1, source_target_pairs={{0,2},{1,3},{2,0},{3,1},{4,6},{5,7},{6,4},{7,5}} | collective-permute-start | bytes 25165832 | tf_op jit(solution)/shard_map/ppermute | solution.py:154
  42.1 360.2 %collective-permute-start.1 = (bf16[4096,1024]{1,0:T(8,128)(2,1)}, bf16[4096,1024]{1,0:T(8,128)(2,1)}, u32[]{:S(2)}, u32[]{:S(2)}) collective-permute-start(bf16[4096,1024]{1,0:T(8,128)(2,1)} %refs_0_.2), channel_id=1, source_target_pairs={{0,2},{1,3},{2,0},{3,1},{4,6},{5,7},{6,4},{7,5}} | collective-permute-start | bytes 25165832 | tf_op jit(solution)/shard_map/ppermute | solution.py:154
  42.1 1485.5 %all-gather.42.cloned.1.call-start = ((), (), s32[]{:S(2)}) async-start(), calls=%async_computation.27 | async-start | bytes 4325376 | tf_op jit(solution)/shard_map/all_gather | solution.py:193
  42.2 555.1 %collective-permute-start.3 = (bf16[4096,1024]{1,0:T(8,128)(2,1)}, bf16[4096,1024]{1,0:T(8,128)(2,1)}, u32[]{:S(2)}, u32[]{:S(2)}) collective-permute-start(bf16[4096,1024]{1,0:T(8,128)(2,1)} %refs_0_.3), channel_id=1, source_target_pairs={{0,1},{1,0},{2,3},{3,2},{4,5},{5,4},{6,7},{7,6}} | collective-permute-start | bytes 25165832 | tf_op jit(solution)/shard_map/ppermute | solution.py:154
  42.2 720.8 %collective-permute-start = (bf16[4096,1024]{1,0:T(8,128)(2,1)}, bf16[4096,1024]{1,0:T(8,128)(2,1)}, u32[]{:S(2)}, u32[]{:S(2)}) collective-permute-start(bf16[4096,1024]{1,0:T(8,128)(2,1)} %refs_0_.2), channel_id=1, source_target_pairs={{0,1},{1,0},{2,3},{3,2},{4,5},{5,4},{6,7},{7,6}} | collective-permute-start | bytes 25165832 | tf_op jit(solution)/shard_map/ppermute | solution.py:154
  60.9 341.6 %copy-start.12 = (f32[4096,6]{0,1:T(8,128)S(1)}, f32[4096,6]{0,1:T(8,128)}, u32[]{:S(2)}) copy-start(f32[4096,6]{0,1:T(8,128)} %param.13) | copy-start | bytes 294916
  223.4 373.9 %collective-permute-start.5 = (bf16[4096,1024]{1,0:T(8,128)(2,1)}, bf16[4096,1024]{1,0:T(8,128)(2,1)}, u32[]{:S(2)}, u32[]{:S(2)}) collective-permute-start(bf16[4096,1024]{1,0:T(8,128)(2,1)} %collective-permute-done.4.refs_2_), channel_id=1, source_target_pairs={{0,1},{1,0},{2,3},{3,2},{4,5},{5,4},{6,7},{7,6}} | collective-permute-start | bytes 25165832 | tf_op jit(solution)/shard_map/ppermute | solution.py:154
  402.3 360.7 %collective-permute-start.2 = (bf16[4096,1024]{1,0:T(8,128)(2,1)}, bf16[4096,1024]{1,0:T(8,128)(2,1)}, u32[]{:S(2)}, u32[]{:S(2)}) collective-permute-start(bf16[4096,1024]{1,0:T(8,128)(2,1)} %collective-permute-done.1.refs_2_), channel_id=1, source_target_pairs={{0,1},{1,0},{2,3},{3,2},{4,5},{5,4},{6,7},{7,6}} | collective-permute-start | bytes 25165832 | tf_op jit(solution)/shard_map/ppermute | solution.py:154
  402.5 318.5 %copy-start.9 = (s32[24576,1]{0,1:T(1,128)}, s32[24576,1]{0,1:T(1,128)S(1)}, u32[]{:S(2)}) copy-start(s32[24576,1]{0,1:T(1,128)S(1)} %compare_select_fusion) | copy-start | bytes 294916
  586.3 9.3 all-to-all-start
  589.8 957.5 %all-gather.40.cloned.1.call-start = ((), (), s32[]{:S(2)}) async-start(), calls=%async_computation.26 | async-start | bytes 4325376 | tf_op jit(solution)/shard_map/all_gather | solution.py:194
  590.3 2538.8 %reduce-scatter.19.cloned.1.call-start = ((), (), s32[]{:S(2)}) async-start(), calls=%async_computation.32 | async-start | bytes 17301504 | tf_op jit(solution)/shard_map/reduce_scatter | solution.py:215
  1038.7 2090.5 %reduce-scatter.17.cloned.1.call-start = ((), (), s32[]{:S(2)}) async-start(), calls=%async_computation.31 | async-start | bytes 17301504 | tf_op jit(solution)/shard_map/reduce_scatter | solution.py:215
  1159.7 1969.5 %reduce-scatter.15.cloned.1.call-start = ((), (), s32[]{:S(2)}) async-start(), calls=%async_computation.30 | async-start | bytes 17301504 | tf_op jit(solution)/shard_map/reduce_scatter | solution.py:215
  1280.9 1848.3 %reduce-scatter.13.cloned.1.call-start = ((), (), s32[]{:S(2)}) async-start(), calls=%async_computation.29 | async-start | bytes 17301504 | tf_op jit(solution)/shard_map/reduce_scatter | solution.py:215
  1401.7 1744.6 %reduce-scatter.27.cloned.1.call-start = ((), (), s32[]{:S(2)}) async-start(), calls=%async_computation.36 | async-start | bytes 17301504 | tf_op jit(solution)/shard_map/reduce_scatter | solution.py:216
  1422.9 1723.4 %reduce-scatter.25.cloned.1.call-start = ((), (), s32[]{:S(2)}) async-start(), calls=%async_computation.35 | async-start | bytes 17301504 | tf_op jit(solution)/shard_map/reduce_scatter | solution.py:216
  1444.5 1701.8 %reduce-scatter.23.cloned.1.call-start = ((), (), s32[]{:S(2)}) async-start(), calls=%async_computation.34 | async-start | bytes 17301504 | tf_op jit(solution)/shard_map/reduce_scatter | solution.py:216
  1465.7 1680.6 %reduce-scatter.21.cloned.1.call-start = ((), (), s32[]{:S(2)}) async-start(), calls=%async_computation.33 | async-start | bytes 17301504 | tf_op jit(solution)/shard_map/reduce_scatter | solution.py:216
  1486.9 1676.5 %reduce-scatter.35.cloned.1.call-start = ((), (), s32[]{:S(2)}) async-start(), calls=%async_computation.40 | async-start | bytes 17301504 | tf_op jit(solution)/shard_map/reduce_scatter | solution.py:217
  1527.6 1635.8 %reduce-scatter.33.cloned.1.call-start = ((), (), s32[]{:S(2)}) async-start(), calls=%async_computation.39 | async-start | bytes 17301504 | tf_op jit(solution)/shard_map/reduce_scatter | solution.py:217
  1647.2 1516.2 %reduce-scatter.31.cloned.1.call-start = ((), (), s32[]{:S(2)}) async-start(), calls=%async_computation.38 | async-start | bytes 17301504 | tf_op jit(solution)/shard_map/reduce_scatter | solution.py:217
  1676.8 7.3 collective-permute-start.10
  1676.8 13.5 collective-permute-start.9
  1686.8 95.4 %collective-permute-start.11 = (f32[3,2,128,1408]{3,2,1,0:T(8,128)}, f32[3,2,128,1408]{3,2,1,0:T(8,128)}, u32[]{:S(2)}, u32[]{:S(2)}) collective-permute-start(f32[3,2,128,1408]{3,2,1,0:T(8,128)} %bitcast_add_fusion), channel_id=1, source_target_pairs={{0,2},{1,3},{2,0},{3,1},{4,6},{5,7},{6,4},{7,5}} | collective-permute-start | bytes 12976136 | tf_op jit(solution)/shard_map/ppermute | solution.py:154
  1791.1 85.8 %collective-permute-start.12 = (f32[3,128,1408]{2,1,0:T(8,128)}, f32[3,128,1408]{2,1,0:T(8,128)S(1)}, u32[]{:S(2)}, u32[]{:S(2)}) collective-permute-start(f32[3,128,1408]{2,1,0:T(8,128)} %dynamic-slice_bitcast_fusion.2), channel_id=1, source_target_pairs={{0,4},{4,0},{1,5},{5,1},{2,6},{6,2},{3,7},{7,3}} | collective-permute-start | bytes 6488072 | tf_op jit(solution)/shard_map/ppermute | solution.py:157
  1880.1 48.5 %collective-permute-start.14 = (f32[3,128,1408]{2,1,0:T(8,128)}, f32[3,128,1408]{2,1,0:T(8,128)}, u32[]{:S(2)}, u32[]{:S(2)}) collective-permute-start(f32[3,128,1408]{2,1,0:T(8,128)} %bitcast_add_fusion.2), channel_id=1, source_target_pairs={{0,2},{1,3},{2,0},{3,1},{4,6},{5,7},{6,4},{7,5}} | collective-permute-start | bytes 6488072 | tf_op jit(solution)/shard_map/ppermute | solution.py:154
  1900.8 1217.8 %collective-permute-start.13 = (f32[3,128,1408]{2,1,0:T(8,128)}, f32[3,128,1408]{2,1,0:T(8,128)}, u32[]{:S(2)}, u32[]{:S(2)}) collective-permute-start(f32[3,128,1408]{2,1,0:T(8,128)} %bitcast_add_fusion.2), channel_id=1, source_target_pairs={{0,1},{1,0},{2,3},{3,2},{4,5},{5,4},{6,7},{7,6}} | collective-permute-start | bytes 6488072 | tf_op jit(solution)/shard_map/ppermute | solution.py:154
  1928.6 1189.9 %collective-permute-start.15 = (f32[3,128,1408]{2,1,0:T(8,128)}, f32[3,128,1408]{2,1,0:T(8,128)}, u32[]{:S(2)}, u32[]{:S(2)}) collective-permute-start(f32[3,128,1408]{2,1,0:T(8,128)} %collective-permute-done.14), channel_id=1, source_target_pairs={{0,1},{1,0},{2,3},{3,2},{4,5},{5,4},{6,7},{7,6}} | collective-permute-start | bytes 6488072 | tf_op jit(solution)/shard_map/ppermute | solution.py:154
  1949.7 1213.8 %reduce-scatter.29.cloned.1.call-start = ((), (), s32[]{:S(2)}) async-start(), calls=%async_computation.37 | async-start | bytes 17301504 | tf_op jit(solution)/shard_map/reduce_scatter | solution.py:217
  2277.4 320.0 %collective-permute-start.7 = (f32[32768,128]{1,0:T(8,128)}, f32[32768,128]{1,0:T(8,128)}, u32[]{:S(2)}, u32[]{:S(2)}) collective-permute-start(f32[32768,128]{1,0:T(8,128)} %get-tuple-element.33), channel_id=1, source_target_pairs={{0,1},{1,0},{2,3},{3,2},{4,5},{5,4},{6,7},{7,6}} | collective-permute-start | bytes 50331656 | tf_op jit(solution)/shard_map/ppermute | solution.py:154
  2323.8 856.8 %collective-permute-start.6 = (f32[32768,128]{1,0:T(8,128)}, f32[32768,128]{1,0:T(8,128)}, u32[]{:S(2)}, u32[]{:S(2)}) collective-permute-start(f32[32768,128]{1,0:T(8,128)} %get-tuple-element.32), channel_id=1, source_target_pairs={{0,1},{1,0},{2,3},{3,2},{4,5},{5,4},{6,7},{7,6}} | collective-permute-start | bytes 50331656 | tf_op jit(solution)/shard_map/ppermute | solution.py:154
  2615.7 564.9 %collective-permute-start.8 = (f32[32768,128]{1,0:T(8,128)}, f32[32768,128]{1,0:T(8,128)}, u32[]{:S(2)}, u32[]{:S(2)}) collective-permute-start(f32[32768,128]{1,0:T(8,128)} %fusion.5), channel_id=1, source_target_pairs={{0,2},{1,3},{2,0},{3,1},{4,6},{5,7},{6,4},{7,5}} | collective-permute-start | bytes 50331656 | tf_op jit(solution)/shard_map/ppermute | solution.py:154
  2682.5 296.9 %all-to-all-start.1 = ((f32[4,16,480]{2,1,0:T(8,128)}), f32[4,16,480]{2,1,0:T(8,128)S(1)}, u32[]{:S(2)}, u32[]{:S(2)}) async-start(f32[4,16,480]{2,1,0:T(8,128)} %pad_maximum_fusion.7), calls=%async_computation.1 | async-start | bytes 262144 | tf_op jit(solution)/shard_map/all_to_all | solution.py:232
  2686.0 293.5 %copy-start.11 = (s32[24576]{0:T(1024)S(1)}, s32[24576]{0:T(1024)}, u32[]{:S(2)}) copy-start(s32[24576]{0:T(1024)} %broadcast_clamp_fusion) | copy-start | bytes 294916
  (29 other events, 927.6 us)
Sparse Core Ops, SparseCore 0:
  15.9 75.0 all-gather.37
  93.0 72.2 all-gather.33
  166.8 72.2 all-gather.35
  240.4 72.2 all-gather.31
  314.0 72.2 all-gather.27
  387.6 72.2 all-gather.29
  462.0 72.2 all-gather.25
  535.7 72.2 all-gather.21
  609.5 72.2 all-gather.23
  683.7 72.2 all-gather.19
  757.5 72.2 all-gather.15
  831.1 72.2 all-gather.17
  904.8 39.1 all-gather.43
  945.4 39.1 all-gather.41
  985.9 39.1 all-gather.39
  1038.8 130.5 reduce-scatter.18
  1171.5 130.3 reduce-scatter.16
  1304.0 130.3 reduce-scatter.14
  1436.7 130.3 reduce-scatter.12
  1569.2 130.3 reduce-scatter.26
  1701.8 167.8 reduce-scatter.24
  1872.0 131.5 reduce-scatter.22
  2005.8 130.3 reduce-scatter.20
  2138.3 130.3 reduce-scatter.34
  2270.9 130.3 reduce-scatter.32
  2403.4 130.3 reduce-scatter.30
  2535.9 130.3 reduce-scatter.28

commit v2 on v1

--- a/solution.py
+++ b/solution.py
@@ -9,7 +9,7 @@
 CAP_DEN = 4
 LANES = 128
 UNROLL = 8
-CHUNKS = 4
+CHUNKS = 2
 
 
 def capacity_for(tok_dev, top_k, n_exp):
@@ -33,9 +33,11 @@
     n_src = len(tables)
     tok_dev, dim = tables[0].shape
     parts = dim // LANES
+    per = n_local // CHUNKS
 
     def body(tok_ref, *refs):
-        tabs, out_ref, raw, wide, rows, sem = refs[:n_src], *refs[n_src:]
+        tabs, outs = refs[:n_src], refs[n_src : n_src + CHUNKS]
+        raw, wide, rows, sem = refs[n_src + CHUNKS :]
         src = pl.program_id(0)
         expert = pl.program_id(1)
 
@@ -64,16 +66,22 @@
                 tok = pl.multiple_of(tok_ref[0, 0, first + slot] * parts, parts)
                 rows[pl.ds(pl.multiple_of(slot * parts, parts), parts), :] = wide[pl.ds(tok, parts), :]
 
-        for j in range(parts):
-            out_ref[0, 0, :, j * LANES : (j + 1) * LANES] = rows[pl.ds(j, capacity, stride=parts), :].astype(out_ref.dtype)
+        for c in range(CHUNKS):
+            @pl.when(expert // per == c)
+            def _():
+                for j in range(parts):
+                    outs[c][0, 0, :, j * LANES : (j + 1) * LANES] = rows[pl.ds(j, capacity, stride=parts), :].astype(outs[c].dtype)
+
+    def block_of(c):
+        return pl.BlockSpec((1, 1, capacity, dim), lambda s, e: (jnp.clip(e - c * per, 0, per - 1), s, 0, 0))
 
     return pl.pallas_call(
         body,
         grid=(n_src, n_local),
         in_specs=[pl.BlockSpec((1, 1, n_local * capacity), lambda s, e: (s, 0, 0), memory_space=pltpu.SMEM)]
         + [pl.BlockSpec(memory_space=pl.ANY)] * n_src,
-        out_specs=pl.BlockSpec((1, 1, capacity, dim), lambda s, e: (e, s, 0, 0)),
-        out_shape=jax.ShapeDtypeStruct((n_local, n_src, capacity, dim), tables[0].dtype),
+        out_specs=[block_of(c) for c in range(CHUNKS)],
+        out_shape=[jax.ShapeDtypeStruct((per, n_src, capacity, dim), tables[0].dtype)] * CHUNKS,
         scratch_shapes=[
             pltpu.VMEM((tok_dev, dim), tables[0].dtype),
             pltpu.VMEM((tok_dev * parts, LANES), jnp.float32),
@@ -86,21 +94,21 @@
     )(tokens.reshape(n_src, 1, n_local * capacity), *tables)
 
 
-def sum_rows(row_chunks, tokens, tok_dev):
+def sum_rows(row_chunks, tokens, source, tok_dev):
     n_chunks = len(row_chunks)
-    per_chunk, n_src, capacity, dim = row_chunks[0].shape
+    per_chunk, _, capacity, dim = row_chunks[0].shape
     n_local = per_chunk * n_chunks
     parts = dim // LANES
 
     def body(tok_ref, *refs):
         chunks, out_ref, wide = refs[:n_chunks], *refs[n_chunks:]
-        step = pl.program_id(1)
+        step = pl.program_id(0)
 
         @pl.when(step == 0)
         def _():
             @pl.loop(0, tok_dev * parts // 256)
             def _(i):
-                out_ref[0, pl.ds(pl.multiple_of(i * 256, 256), 256), :] = jnp.zeros((256, LANES), jnp.float32)
+                out_ref[pl.ds(pl.multiple_of(i * 256, 256), 256), :] = jnp.zeros((256, LANES), jnp.float32)
 
         for c in range(n_chunks):
             for j in range(parts):
@@ -112,25 +120,25 @@
                 where, sums = [], []
                 for k in range(UNROLL):
                     slot = i * UNROLL + k
-                    tok = pl.multiple_of(tok_ref[0, 0, first + slot] * parts, parts)
+                    tok = pl.multiple_of(tok_ref[0, first + slot] * parts, parts)
                     where.append(tok)
                     row = wide[pl.ds(pl.multiple_of(slot * parts, parts), parts), :]
-                    sums.append(out_ref[0, pl.ds(tok, parts), :] + row)
+                    sums.append(out_ref[pl.ds(tok, parts), :] + row)
                 for k in reversed(range(UNROLL)):
-                    out_ref[0, pl.ds(where[k], parts), :] = sums[k]
+                    out_ref[pl.ds(where[k], parts), :] = sums[k]
 
     return pl.pallas_call(
         body,
-        grid=(n_src, per_chunk),
-        in_specs=[pl.BlockSpec((1, 1, n_local * capacity), lambda s, e: (s, 0, 0), memory_space=pltpu.SMEM)]
-        + [pl.BlockSpec((1, 1, capacity, dim), lambda s, e: (e, s, 0, 0))] * n_chunks,
-        out_specs=pl.BlockSpec((1, tok_dev * parts, LANES), lambda s, e: (s, 0, 0)),
-        out_shape=jax.ShapeDtypeStruct((n_src, tok_dev * parts, LANES), jnp.float32),
+        grid=(per_chunk,),
+        in_specs=[pl.BlockSpec((1, n_local * capacity), lambda e: (0, 0), memory_space=pltpu.SMEM)]
+        + [pl.BlockSpec((1, 1, capacity, dim), lambda e: (e, source, 0, 0))] * n_chunks,
+        out_specs=pl.BlockSpec((tok_dev * parts, LANES), lambda e: (0, 0)),
+        out_shape=jax.ShapeDtypeStruct((tok_dev * parts, LANES), jnp.float32),
         scratch_shapes=[pltpu.VMEM((capacity * parts, LANES), jnp.float32)],
         compiler_params=pltpu.CompilerParams(vmem_limit_bytes=56 * 2**20),
-        cost_estimate=pl.CostEstimate(flops=600_000_000, bytes_accessed=130_000_000, transcendentals=0),
+        cost_estimate=pl.CostEstimate(flops=150_000_000, bytes_accessed=32_000_000, transcendentals=0),
         name="sum_rows",
-    )(tokens.reshape(n_src, 1, n_local * capacity), *row_chunks)
+    )(tokens.reshape(1, n_local * capacity), *row_chunks)
 
 
 def swiglu_hidden(h_one, h_three, d_act):
@@ -152,6 +160,9 @@
 
     def swap(value, bit):
         return lax.ppermute(value, "ep", [(i, i ^ bit) for i in range(ep_size)])
+
+    def tie(*values):
+        return lax.optimization_barrier(values)
 
     def swap_fs(value):
         return lax.ppermute(value, "fsdp", [(i, i ^ 1) for i in range(fs_size)])
@@ -166,16 +177,17 @@
         row = lax.axis_index("fsdp")
         pick = lambda a, i, axis=0: lax.dynamic_index_in_dim(a, i, axis, keepdims=False)
 
-        def spread(value):
-            across = swap(value, 2)
-            return [value, swap(value, 1), across, swap(across, 1)]
-
-        x_tabs = spread(x_loc)
-        dy_tabs = spread(dy_loc)
+        def spread(value, near, across):
+            return [value, near, across, swap(across, 1)]
+
+        x_near, x_across = swap(x_loc, 1), swap(x_loc, 2)
+        dy_near, dy_across = swap(dy_loc, 1), swap(dy_loc, 2)
 
         slot_idx, slot_tok, slot_gate = route_slots(ids_loc, gate_loc, n_exp, capacity)
         table = jnp.stack([slot_tok.astype(jnp.float32), slot_gate]).reshape(2, ep_size, n_local, capacity).swapaxes(0, 1)
+        table, x_across = tie(table, x_across)
         table = lax.all_to_all(table, "ep", 0, 0, tiled=True)
+        x_tabs = spread(x_loc, x_near, x_across)
         table = jnp.stack([pick(table, me ^ m) for m in range(ep_size)])
         tokens = table[:, 0].astype(jnp.int32)
         gates = table[:, 1].swapaxes(0, 1).reshape(n_local, ep_size * capacity, 1)
@@ -193,16 +205,17 @@
         ws_three_full = lax.all_gather(ws_three, "fsdp", axis=0, tiled=True)
         ws_two_full = lax.all_gather(ws_two, "fsdp", axis=1, tiled=True)
 
-        x_rows = gather_rows(x_tabs, tokens, n_local, capacity).reshape(n_local, ep_size * capacity, model_dim)
-        dy_rows = gather_rows(dy_tabs, tokens, n_local, capacity).reshape(n_local, ep_size * capacity, model_dim)
-
-        dx_chunks, dgate_chunks, grads = [], [], []
+        x_rows = [r.reshape(per, ep_size * capacity, model_dim) for r in gather_rows(x_tabs, tokens, n_local, capacity)]
+        x_rows[0], dy_across = tie(x_rows[0], dy_across)
+        dy_tabs = spread(dy_loc, dy_near, dy_across)
+        dy_rows = [r.reshape(per, ep_size * capacity, model_dim) for r in gather_rows(dy_tabs, tokens, n_local, capacity)]
+
+        dx_chunks, acts, grads = [], [], []
         for c in range(CHUNKS):
             part = slice(c * per, (c + 1) * per)
             w_a, w_c, w_b = weights[c]
-            x_c, gate_c = x_rows[part], gates[part]
-            dy_c = dy_rows[part].astype(jnp.float32)
-            g_c = (gate_c * dy_c).astype(jnp.bfloat16)
+            x_c, dy_c, gate_c = x_rows[c], dy_rows[c], gates[part]
+            g_c = (gate_c * dy_c.astype(jnp.float32)).astype(jnp.bfloat16)
             h_one = dot32("erd,edf->erf", x_c, w_a)
             h_three = dot32("erd,edf->erf", x_c, w_c)
             d_act = dot32("erd,efd->erf", g_c, w_b)
@@ -211,22 +224,28 @@
             dw_two = dot32("erf,erd->efd", act, g_c)
             dw_one = dot32("erd,erf->edf", x_c, dh_one)
             dw_three = dot32("erd,erf->edf", x_c, dh_three)
+            dx_c = (dot32("erf,edf->erd", dh_one, w_a) + dot32("erf,edf->erd", dh_three, w_c)).astype(jnp.bfloat16)
+            if c + 1 < CHUNKS:
+                x_rows[c + 1], dy_rows[c + 1], dw_one, dw_two, dw_three, dx_c = tie(x_rows[c + 1], dy_rows[c + 1], dw_one, dw_two, dw_three, dx_c)
             grads.append((
                 lax.psum_scatter(dw_one, "fsdp", scatter_dimension=1, tiled=True),
                 lax.psum_scatter(dw_two, "fsdp", scatter_dimension=2, tiled=True),
                 lax.psum_scatter(dw_three, "fsdp", scatter_dimension=1, tiled=True),
             ))
-            dx_c = (dot32("erf,edf->erd", dh_one, w_a) + dot32("erf,edf->erd", dh_three, w_c)).astype(jnp.bfloat16)
             dx_chunks.append(dx_c.reshape(per, ep_size, capacity, model_dim))
-            y_c = dot32("erf,efd->erd", act, w_b)
-            dgate_chunks.append(jnp.sum(dy_c * y_c, axis=-1))
-
-        dx_part = sum_rows(dx_chunks, tokens, tok_dev)
+            acts.append(act)
+
+        dx_part = {m: sum_rows(dx_chunks, tokens[m], m, tok_dev) for m in (3, 1, 2, 0)}
         from_core = swap(dx_part[3], 1)
+        dx_near = swap(dx_part[1], 1)
+        dx_part[0], x_loc, dy_loc, *acts = tie(dx_part[0], x_loc, dy_loc, *acts)
         to_chip = dx_part[2] + from_core
         from_chip = swap(to_chip, 2)
-        dx_near = swap(dx_part[1], 1)
-
+
+        dgate_chunks = [
+            jnp.sum(acts[c].astype(jnp.float32) * dot32("erd,efd->erf", dy_rows[c], weights[c][2]), axis=-1)
+            for c in range(CHUNKS)
+        ]
         dgate = jnp.concatenate(dgate_chunks).reshape(n_local, ep_size, capacity).swapaxes(0, 1)
         dgate = jnp.stack([pick(dgate, me ^ k) for k in range(ep_size)])
         dgate = lax.all_to_all(dgate, "ep", 0, 0, tiled=True).reshape(-1)
@@ -245,12 +264,14 @@
         far = by_place[2] + swap(by_place[3], 1)
         near = near + swap(far, 2)
         mine = pick(near, row, 1) + swap_fs(pick(near, row ^ 1, 1))
-        pieces = jnp.stack(spread(mine), axis=1)
+        pieces = jnp.stack(spread(mine, swap(mine, 1), swap(mine, 2)), axis=1)
         pieces = jnp.stack([pick(pieces, me ^ k, 1) for k in range(ep_size)], axis=1).reshape(3, model_dim // fs_size, sff)
 
         total = (dx_part[0] + dx_near) + from_chip
         dx_loc = (total.reshape(tok_dev, model_dim) + dx_shared.astype(jnp.float32)).astype(jnp.bfloat16)
-        dw_one, dw_two, dw_three = [jnp.concatenate([g[i] for g in grads]) for i in range(3)]
+        dw_one, dw_two, dw_three = [jnp.zeros((n_local,) + grads[0][i].shape[1:], jnp.float32) for i in range(3)]
+        for c in range(CHUNKS):
+            dw_one, dw_two, dw_three = [lax.dynamic_update_slice(a, g, (c * per, 0, 0)) for a, g in zip((dw_one, dw_two, dw_three), grads[c])]
         return dx_loc, dgate_loc, dw_one, dw_two, dw_three, pieces[0], pieces[1].T, pieces[2]
 
     return jax.shard_map(device_step, mesh=mesh, in_specs=in_specs, out_specs=out_specs, check_vma=False)

time: 3250 us -> 2660 us (0.82)
  local copies, waits for them, and re-layouts: 650 us -> 420 us
  other arithmetic: 326 us -> 151 us
  waiting for transfers between devices: 821 us -> 701 us
  matrix products: 1050 us -> 958 us
    all_to_all x1, waiting for transfers between devices: 272 us -> 0.01 us  [device_step(): dgate = lax.all_to_all(dgate, 'ep', 0, 0, tiled=True).reshape(-1)]
    reduce_scatter x4 -> x2, waiting for transfers between devices: 0.02 us -> 215 us  [device_step(): lax.psum_scatter(dw_one, 'fsdp', scatter_dimension=1, tiled=True)]
    ppermute x15, waiting for transfers between devices: 453 us -> 263 us  [swap(): return lax.ppermute(value, 'ep', [(i, i ^ bit) for i in range(ep_size)])]
    all_to_all x1, waiting for transfers between devices: 5.21 us -> 179 us  [device_step(): table = lax.all_to_all(table, 'ep', 0, 0, tiled=True)]
    convert_element_type x4 -> x0, local copies, waits for them, and re-layouts: 123 us -> none  [device_step(): dy_c = dy_rows[part].astype(jnp.float32)]
    convert_element_type x8 -> x0, other arithmetic: 114 us -> none  [the longest x4 63.4 us: device_step(): dy_c = dy_rows[part].astype(jnp.float32)]
    dot_general x44 -> x26, matrix products: 1050 us -> 958 us  [dot32(): return jnp.einsum(form, a, b, preferred_element_type=jnp.float32)]
    slice x11 -> x6, local copies, waits for them, and re-layouts: 79.8 us -> 1.61 us  [the longest x5 0.98 us: device_step(): x_c, dy_c, gate_c = (x_rows[c], dy_rows[c], gates[part])]
  transfers between devices with their start and end apart: 45 -> 33, of which waited for: 9 -> 5; matrix products, arithmetic and copies ran while one was open for 60% -> 56% of each run, Pallas kernels for 11% -> 15%
where the time goes in v2:
time: 2660 us; the launch traced here: 2650 us
  matrix products  958 us (36%)
  waiting for transfers between devices  701 us (26%)
  local copies, waits for them, and re-layouts  420 us (16%)
  Pallas kernels  389 us (15%)
  other arithmetic  151 us (6%)
    dot_general x26, matrix products, dot32(): return jnp.einsum(form, a, b, preferred_element_type=jnp.float32)  958 us
    ppermute x15, waiting for transfers between devices, swap(): return lax.ppermute(value, 'ep', [(i, i ^ bit) for i in range(ep_size)])  263 us
    pallas_call x2, Pallas kernels, gather_rows(): pl.pallas_call(body, grid=(n_src, n_local), in_specs=[pl.BlockSpec((1, 1,...  247 us
    reduce_scatter x2, waiting for transfers between devices, device_step(): lax.psum_scatter(dw_one, 'fsdp', scatter_dimension=1, tiled=True)  215 us
    all_to_all x1, waiting for transfers between devices, device_step(): table = lax.all_to_all(table, 'ep', 0, 0, tiled=True)  179 us
    pallas_call x4, Pallas kernels, sum_rows(): pl.pallas_call(body, grid=(per_chunk,), in_specs=[pl.BlockSpec((1, n_loca...  141 us
    gather x1, local copies, waits for them, and re-layouts, device_step(): jnp.concatenate([dgate, jnp.zeros((1,), jnp.float32)])[slot_idx]  136 us
    scatter x1, local copies, waits for them, and re-layouts, route_slots(): jnp.zeros((n_exp * capacity + 1,), jnp.float32).at[slot_idx]  90.3 us
  transfers between devices with their start and end apart: 33, of which 5 were waited for; matrix products, arithmetic and copies ran while one was open for 56% of the time, Pallas kernels for 15%

profile of v2, /device:TPU:0, one launch (start us, length us, event | category | flops | bytes accessed | tf_op | source)
XLA Modules:
  0.0 2651.6 jit_solution(2482892641475275733)
XLA Ops:
  7.2 9.8 fusion.25
  17.1 9.6 fusion.23
  80.5 90.3 %scatter_custom_fusion.1 = f32[30721]{0:T(1024)S(1)} fusion(s32[24576]{0:T(1024)S(1)} %bitcast.156, f32[24576]{0:T(1024)S(1)} %reshape.222, f32[]{:T(128)} %constant.90.clone.1), kind=kCustom, calls=%fused_computation.79 | custom fusion | bytes 122888 | tf_op jit(solution)/shard_map/scatter | solution.py:28
  171.0 90.3 %scatter_custom_fusion = s32[30721]{0:T(1024)S(1)} fusion(s32[24576]{0:T(1024)S(1)} %bitcast.157, s32[24576]{0:T(1024)S(1)} %add_select_fusion, s32[]{:T(128)} %constant.83.clone.1), kind=kCustom, calls=%fused_computation.81 | custom fusion | bytes 122888 | tf_op jit(solution)/shard_map/scatter | solution.py:27
  267.6 179.5 %all-to-all-done = f32[4,2,16,480]{3,2,1,0:T(8,128)S(1)} async-done(((f32[4,2,16,480]{3,2,1,0:T(8,128)}), f32[4,2,16,480]{3,2,1,0:T(8,128)S(1)}, u32[]{:S(2)}, u32[]{:S(2)}) %all-to-all-start) | async-done | bytes 245792 | tf_op jit(solution)/shard_map/all_to_all | solution.py:189
  451.6 123.9 %gather_rows.2 = (bf16[8,4,480,1024]{3,2,1,0:T(8,128)(2,1)}, bf16[8,4,480,1024]{3,2,1,0:T(8,128)(2,1)}) custom-call(s32[4,1,7680]{2,1,0:T(1,128)S(1)} %convert_element_type.94.tok_ref, bf16[4096,1024]{1,0:T(8,128)(2,1)S(1)} %copy-done, bf16[4096,1024]{1,0:T(8,128)(2,1)} %collective-permute-done.1.refs_1_, bf16[4096,1024]{1,0:T(8,128)(2,1)} %collective-permute-done.refs_2_, ...), custom_call_target="tpu_custom_call" | custom-call | flops 600000000 | bytes 100000000 | tf_op jit(solution)/shard_map/gather_rows/pallas_call | solution.py:78
  575.6 40.5 %fusion.30 = f32[8,1920,704]{1,2,0:T(8,128)} fusion(bf16[8,1920,1024]{2,1,0:T(8,128)(2,1)} %bitcast.171, bf16[8,1024,704]{1,2,0:T(8,128)(2,1)} %all-gather.14.cloned.1.call-done), kind=kOutput, calls=%fused_computation.111 | convolution fusion | flops 22145925120 | bytes 86245376 | tf_op jit(solution)/shard_map/erd,edf->erf/dot_general | solution.py:151
  616.1 40.5 %fusion.29 = f32[8,1920,704]{1,2,0:T(8,128)} fusion(bf16[8,1920,1024]{2,1,0:T(8,128)(2,1)} %bitcast.172, bf16[8,1024,704]{1,2,0:T(8,128)(2,1)} %all-gather.12.cloned.1.call-done), kind=kOutput, calls=%fused_computation.110 | convolution fusion | flops 22145925120 | bytes 86245376 | tf_op jit(solution)/shard_map/erd,edf->erf/dot_general | solution.py:151
  660.0 123.6 %gather_rows.3 = (bf16[8,4,480,1024]{3,2,1,0:T(8,128)(2,1)}, bf16[8,4,480,1024]{3,2,1,0:T(8,128)(2,1)}) custom-call(s32[4,1,7680]{2,1,0:T(1,128)S(1)} %convert_element_type.94.tok_ref, bf16[4096,1024]{1,0:T(8,128)(2,1)S(1)} %copy-done.1, bf16[4096,1024]{1,0:T(8,128)(2,1)} %collective-permute-done.3.refs_1_, ...), custom_call_target="tpu_custom_call" | custom-call | flops 600000000 | bytes 100000000 | tf_op jit(solution)/shard_map/gather_rows/pallas_call | solution.py:78
  783.6 71.0 %select_convert_fusion.3 = (bf16[8,1920,704]{1,2,0:T(8,128)(2,1)}, bf16[8,1920,704]{1,2,0:T(8,128)(2,1)}, bf16[8,1920,704]{1,2,0:T(8,128)(2,1)}) fusion(pred[8,1920]{1,0:T(8,128)(4,1)S(1)} %broadcast_compare_fusion.1, f32[8,1920,704]{1,2,0:T(8,128)} %fusion.30, f32[8,1920,704]{1,2,0:T(8,128)} %fusion.29, ...), kind=kOutput, calls=%fused_computation.14 | convolution fusion | flops 22387752960 | bytes 194456576 | tf_op jit(solution)/shard_map/erd,efd->erf/dot_general | solution.py:151
  854.6 37.9 %fusion.2 = f32[8,704,1024]{2,1,0:T(8,128)} fusion(bf16[8,1920,704]{1,2,0:T(8,128)(2,1)} %get-tuple-element.41, bf16[8,1920,1024]{2,1,0:T(8,128)(2,1)} %bitcast.162, f32[8,1920]{1,0:T(8,128)S(1)} %slice.96), kind=kOutput, calls=%fused_computation.19 | convolution fusion | flops 22193111040 | bytes 76214272 | tf_op jit(solution)/shard_map/erf,erd->efd/dot_general | solution.py:151
  892.5 37.8 %fusion.40 = f32[8,1024,704]{1,2,0:T(8,128)} fusion(bf16[8,1920,704]{1,2,0:T(8,128)(2,1)} %get-tuple-element.73, bf16[8,1920,1024]{2,1,0:T(8,128)(2,1)} %bitcast.173), kind=kOutput, calls=%fused_computation.121 | convolution fusion | flops 22145925120 | bytes 76152832 | tf_op jit(solution)/shard_map/erd,erf->edf/dot_general | solution.py:151
  930.3 38.1 %fusion.31 = f32[8,1920,1024]{2,1,0:T(8,128)} fusion(bf16[8,1920,704]{1,2,0:T(8,128)(2,1)} %get-tuple-element.74, bf16[8,1024,704]{1,2,0:T(8,128)(2,1)} %all-gather.14.cloned.1.call-done), kind=kOutput, calls=%fused_computation.112 | convolution fusion | flops 22145925120 | bytes 96075776 | tf_op jit(solution)/shard_map/erf,edf->erd/dot_general | solution.py:151
  968.4 48.4 %add_convert_fusion.1 = bf16[8,1920,1024]{2,1,0:T(8,128)(2,1)} fusion(f32[8,1920,1024]{2,1,0:T(8,128)} %fusion.31, bf16[8,1920,704]{1,2,0:T(8,128)(2,1)} %get-tuple-element.73, bf16[8,1024,704]{1,2,0:T(8,128)(2,1)} %all-gather.12.cloned.1.call-done), kind=kOutput, calls=%fused_computation.5 | convolution fusion | flops 22177382400 | bytes 127533056 | tf_op jit(solution)/shard_map/erf,edf->erd/dot_general | solution.py:151
  1016.8 37.7 %fusion.39 = f32[8,1024,704]{1,2,0:T(8,128)} fusion(bf16[8,1920,704]{1,2,0:T(8,128)(2,1)} %get-tuple-element.74, bf16[8,1920,1024]{2,1,0:T(8,128)(2,1)} %bitcast.174), kind=kOutput, calls=%fused_computation.120 | convolution fusion | flops 22145925120 | bytes 76152832 | tf_op jit(solution)/shard_map/erd,erf->edf/dot_general | solution.py:151
  1055.6 40.7 %fusion.32 = f32[8,1920,704]{1,2,0:T(8,128)} fusion(bf16[8,1920,1024]{2,1,0:T(8,128)(2,1)} %bitcast.167, bf16[8,1024,704]{1,2,0:T(8,128)(2,1)} %all-gather.20.cloned.1.call-done), kind=kOutput, calls=%fused_computation.113 | convolution fusion | flops 22145925120 | bytes 86245376 | tf_op jit(solution)/shard_map/erd,edf->erf/dot_general | solution.py:151
  1096.3 40.9 %fusion.5 = f32[8,1920,704]{1,2,0:T(8,128)} fusion(bf16[8,704,1024]{2,1,0:T(8,128)(2,1)} %all-gather.16.cloned.1.call-done, bf16[8,1920,1024]{2,1,0:T(8,128)(2,1)} %bitcast.164, f32[8,1920]{1,0:T(8,128)S(1)} %slice.101), kind=kOutput, calls=%fused_computation.22 | convolution fusion | flops 22193111040 | bytes 86306816 | tf_op jit(solution)/shard_map/erd,efd->erf/dot_general | solution.py:151
  1137.2 70.5 %select_convert_fusion = (bf16[8,1920,704]{1,2,0:T(8,128)(2,1)}, bf16[8,1920,704]{1,2,0:T(8,128)(2,1)}, bf16[8,1920,704]{1,2,0:T(8,128)(2,1)}) fusion(pred[8,1920]{1,0:T(8,128)(4,1)S(1)} %broadcast_compare_fusion, f32[8,1920,704]{1,2,0:T(8,128)} %fusion.32, f32[8,1920,704]{1,2,0:T(8,128)} %fusion.5, bf16[8,1920,1024]{2,1,0:T(8,128)(2,1)} %bitcast.168, ...), kind=kOutput, calls=%fused_computation.9 | convolution fusion | flops 22340567040 | bytes 194395136 | tf_op jit(solution)/shard_map/erd,edf->erf/dot_general | solution.py:151
  1207.7 38.0 %fusion.4 = f32[8,704,1024]{2,1,0:T(8,128)} fusion(bf16[8,1920,704]{1,2,0:T(8,128)(2,1)} %get-tuple-element.42, bf16[8,1920,1024]{2,1,0:T(8,128)(2,1)} %bitcast.165, f32[8,1920]{1,0:T(8,128)S(1)} %slice.101), kind=kOutput, calls=%fused_computation.21 | convolution fusion | flops 22193111040 | bytes 76214272 | tf_op jit(solution)/shard_map/erf,erd->efd/dot_general | solution.py:151
  1246.4 37.9 %fusion.42 = f32[8,1024,704]{1,2,0:T(8,128)} fusion(bf16[8,1920,704]{1,2,0:T(8,128)(2,1)} %get-tuple-element.72, bf16[8,1920,1024]{2,1,0:T(8,128)(2,1)} %bitcast.169), kind=kOutput, calls=%fused_computation.123 | convolution fusion | flops 22145925120 | bytes 76152832 | tf_op jit(solution)/shard_map/erd,erf->edf/dot_general | solution.py:151
  1287.3 38.1 %fusion.33 = f32[8,1920,1024]{2,1,0:T(8,128)} fusion(bf16[8,1920,704]{1,2,0:T(8,128)(2,1)} %get-tuple-element.71, bf16[8,1024,704]{1,2,0:T(8,128)(2,1)} %all-gather.20.cloned.1.call-done), kind=kOutput, calls=%fused_computation.114 | convolution fusion | flops 22145925120 | bytes 96075776 | tf_op jit(solution)/shard_map/erf,edf->erd/dot_general | solution.py:151
  1325.3 48.4 %add_convert_fusion = bf16[8,1920,1024]{2,1,0:T(8,128)(2,1)} fusion(f32[8,1920,1024]{2,1,0:T(8,128)} %fusion.33, bf16[8,1920,704]{1,2,0:T(8,128)(2,1)} %get-tuple-element.72, bf16[8,1024,704]{1,2,0:T(8,128)(2,1)} %all-gather.18.cloned.1.call-done), kind=kOutput, calls=%fused_computation.3 | convolution fusion | flops 22177382400 | bytes 127533056 | tf_op jit(solution)/shard_map/erf,edf->erd/dot_general | solution.py:151
  1373.7 35.2 %sum_rows.4 = f32[32768,128]{1,0:T(8,128)} custom-call(s32[1,7680]{1,0:T(1,128)} %reshape_squeeze.12.tok_ref, bf16[8,4,480,1024]{3,2,1,0:T(8,128)(2,1)} %bitcast.139, bf16[8,4,480,1024]{3,2,1,0:T(8,128)(2,1)} %bitcast.143), custom_call_target="tpu_custom_call" | custom-call | flops 150000000 | bytes 32000000 | tf_op jit(solution)/shard_map/sum_rows/pallas_call | solution.py:130
  1408.9 35.2 %sum_rows.7 = f32[32768,128]{1,0:T(8,128)} custom-call(s32[1,7680]{1,0:T(1,128)} %reshape_squeeze.15.tok_ref, bf16[8,4,480,1024]{3,2,1,0:T(8,128)(2,1)} %bitcast.140, bf16[8,4,480,1024]{3,2,1,0:T(8,128)(2,1)} %bitcast.144), custom_call_target="tpu_custom_call" | custom-call | flops 150000000 | bytes 32000000 | tf_op jit(solution)/shard_map/sum_rows/pallas_call | solution.py:130
  1444.6 19.6 fusion.35
  1464.2 19.5 fusion.34
  1483.7 33.7 %multiply_convert_fusion.7 = (bf16[4096,1408]{1,0:T(8,128)(2,1)}, bf16[4096,1408]{1,0:T(8,128)(2,1)}) fusion(f32[4096,1408]{1,0:T(8,128)} %fusion.35, f32[4096,1408]{1,0:T(8,128)} %fusion.34, bf16[4096,1024]{1,0:T(8,128)(2,1)} %refs_0_.3, bf16[1408,1024]{1,0:T(8,128)(2,1)} %all-gather.22.cloned.1.call-done), kind=kOutput, calls=%fused_computation.27 | convolution fusion | flops 11886133248 | bytes 80478208 | tf_op jit(solution)/shard_map/td,fd->tf/dot_general | solution.py:151
  1517.4 19.6 fusion.38
  1537.0 37.9 %fusion.41 = f32[8,1024,704]{1,2,0:T(8,128)} fusion(bf16[8,1920,704]{1,2,0:T(8,128)(2,1)} %get-tuple-element.71, bf16[8,1920,1024]{2,1,0:T(8,128)(2,1)} %bitcast.170), kind=kOutput, calls=%fused_computation.122 | convolution fusion | flops 22145925120 | bytes 76152832 | tf_op jit(solution)/shard_map/erd,erf->edf/dot_general | solution.py:151
  1574.9 19.5 fusion.37
  1594.4 24.5 fusion.7
  1651.8 35.2 %sum_rows.5 = f32[32768,128]{1,0:T(8,128)} custom-call(s32[1,7680]{1,0:T(1,128)} %reshape_squeeze.13.tok_ref, bf16[8,4,480,1024]{3,2,1,0:T(8,128)(2,1)} %bitcast.141, bf16[8,4,480,1024]{3,2,1,0:T(8,128)(2,1)} %bitcast.145), custom_call_target="tpu_custom_call" | custom-call | flops 150000000 | bytes 32000000 | tf_op jit(solution)/shard_map/sum_rows/pallas_call | solution.py:130
  1687.0 35.6 %sum_rows.6 = f32[32768,128]{1,0:T(8,128)} custom-call(s32[1,7680]{1,0:T(1,128)} %reshape_squeeze.14.tok_ref, bf16[8,4,480,1024]{3,2,1,0:T(8,128)(2,1)} %bitcast.142, bf16[8,4,480,1024]{3,2,1,0:T(8,128)(2,1)} %bitcast.146), custom_call_target="tpu_custom_call" | custom-call | flops 150000000 | bytes 32000000 | tf_op jit(solution)/shard_map/sum_rows/pallas_call | solution.py:130
  1722.5 17.8 add.147
  1741.9 38.3 %multiply_reduce_fusion = f32[8,1920]{1,0:T(8,128)S(1)} fusion(bf16[8,1920,704]{1,2,0:T(8,128)(2,1)} %get-tuple-element.42, bf16[8,1920,1024]{2,1,0:T(8,128)(2,1)} %bitcast.166, bf16[8,704,1024]{2,1,0:T(8,128)(2,1)} %all-gather.16.cloned.1.call-done), kind=kOutput, calls=%fused_computation.7 | convolution fusion | flops 22178349056 | bytes 64679936 | tf_op jit(solution)/shard_map/erd,efd->erf/dot_general | solution.py:151
  1789.3 38.2 %multiply_reduce_fusion.1 = f32[8,1920]{1,0:T(8,128)S(1)} fusion(bf16[8,1920,704]{1,2,0:T(8,128)(2,1)} %get-tuple-element.41, bf16[8,1920,1024]{2,1,0:T(8,128)(2,1)} %bitcast.163, bf16[8,704,1024]{2,1,0:T(8,128)(2,1)} %all-gather.10.cloned.1.call-done), kind=kOutput, calls=%fused_computation.8 | convolution fusion | flops 22178349056 | bytes 64679936 | tf_op jit(solution)/shard_map/erd,efd->erf/dot_general | solution.py:151
  1832.1 41.0 %collective-permute-done.12 = f32[3,128,1408]{2,1,0:T(8,128)} collective-permute-done((f32[3,128,1408]{2,1,0:T(8,128)S(1)}, f32[3,128,1408]{2,1,0:T(8,128)}, u32[]{:S(2)}, u32[]{:S(2)}) %collective-permute-start.12) | collective-permute-done | bytes 2162720 | tf_op jit(solution)/shard_map/ppermute | solution.py:168
  1877.0 19.2 fusion.36
  1896.2 255.8 %collective-permute-done.14 = f32[3,128,1408]{2,1,0:T(8,128)} collective-permute-done((f32[3,128,1408]{2,1,0:T(8,128)S(1)}, f32[3,128,1408]{2,1,0:T(8,128)}, u32[]{:S(2)}, u32[]{:S(2)}) %collective-permute-start.14) | collective-permute-done | bytes 2162720 | tf_op jit(solution)/shard_map/ppermute | solution.py:162
  2152.0 21.4 add_convert_fusion.3
  2173.6 135.5 %gather_fusion = f32[24576]{0:T(1024)S(1)} fusion(f32[30721]{0:T(1024)S(1)} %pad_maximum_fusion.8, s32[24576]{0:T(1024)S(1)} %copy-done.9), kind=kCustom, calls=%fused_computation | custom fusion | bytes 294912 | tf_op jit(solution)/shard_map/gather | solution.py:252
  2325.8 22.7 add_add_fusion
  2348.5 18.0 reshape.198
  2366.5 12.0 add_convert_fusion.2
  2378.4 17.1 pad_maximum_fusion.1
  2395.6 17.1 pad_maximum_fusion.2
  2412.7 214.8 %reduce-scatter.9.cloned.1.call-done = f32[8,512,704]{1,2,0:T(8,128)} async-done(((f32[8,1024,704]{1,2,0:T(8,128)}), f32[8,512,704]{1,2,0:T(8,128)}) %reduce-scatter.9.cloned.1.call-update) | async-done | bytes 11534352 | tf_op jit(solution)/shard_map/reduce_scatter | solution.py:231
  2627.5 17.1 pad_maximum_fusion
  (174 shorter events, 141.9 us)
Async XLA Ops:
  7.2 568.4 %all-gather.14.cloned.1.call-start = ((), (), s32[]{:S(2)}) async-start(), calls=%async_computation.10 | async-start | bytes 17301504 | tf_op jit(solution)/shard_map/all_gather | solution.py:200
  17.0 599.1 %all-gather.12.cloned.1.call-start = ((), (), s32[]{:S(2)}) async-start(), calls=%async_computation.9 | async-start | bytes 17301504 | tf_op jit(solution)/shard_map/all_gather | solution.py:201
  26.7 756.9 %all-gather.10.cloned.1.call-start = ((), (), s32[]{:S(2)}) async-start(), calls=%async_computation.8 | async-start | bytes 17301504 | tf_op jit(solution)/shard_map/all_gather | solution.py:202
  36.3 4.7 copy-start.6
  36.3 1019.3 %all-gather.20.cloned.1.call-start = ((), (), s32[]{:S(2)}) async-start(), calls=%async_computation.13 | async-start | bytes 17301504 | tf_op jit(solution)/shard_map/all_gather | solution.py:200
  36.9 14.8 copy-start.11
  36.9 1059.4 %all-gather.16.cloned.1.call-start = ((), (), s32[]{:S(2)}) async-start(), calls=%async_computation.11 | async-start | bytes 17301504 | tf_op jit(solution)/shard_map/all_gather | solution.py:202
  37.5 1099.7 %all-gather.18.cloned.1.call-start = ((), (), s32[]{:S(2)}) async-start(), calls=%async_computation.12 | async-start | bytes 17301504 | tf_op jit(solution)/shard_map/all_gather | solution.py:201
  37.6 410.7 %collective-permute-start.1 = (bf16[4096,1024]{1,0:T(8,128)(2,1)}, bf16[4096,1024]{1,0:T(8,128)(2,1)}, u32[]{:S(2)}, u32[]{:S(2)}) collective-permute-start(bf16[4096,1024]{1,0:T(8,128)(2,1)} %refs_0_.2), channel_id=1, source_target_pairs={{0,1},{1,0},{2,3},{3,2},{4,5},{5,4},{6,7},{7,6}} | collective-permute-start | bytes 25165832 | tf_op jit(solution)/shard_map/ppermute | solution.py:162
  38.4 223.0 %collective-permute-start = (bf16[4096,1024]{1,0:T(8,128)(2,1)}, bf16[4096,1024]{1,0:T(8,128)(2,1)}, u32[]{:S(2)}, u32[]{:S(2)}) collective-permute-start(bf16[4096,1024]{1,0:T(8,128)(2,1)} %refs_0_.2), channel_id=1, source_target_pairs={{0,2},{1,3},{2,0},{3,1},{4,6},{5,7},{6,4},{7,5}} | collective-permute-start | bytes 25165832 | tf_op jit(solution)/shard_map/ppermute | solution.py:162
  41.0 1403.6 %all-gather.26.cloned.1.call-start = ((), (), s32[]{:S(2)}) async-start(), calls=%async_computation.16 | async-start | bytes 4325376 | tf_op jit(solution)/shard_map/all_gather | solution.py:204
  80.5 180.7 %copy-start.7 = (s32[24576,1]{0,1:T(1,128)}, s32[24576,1]{0,1:T(1,128)S(1)}, u32[]{:S(2)}) copy-start(s32[24576,1]{0,1:T(1,128)S(1)} %compare_select_fusion) | copy-start | bytes 294916
  261.4 186.8 %collective-permute-start.2 = (bf16[4096,1024]{1,0:T(8,128)(2,1)}, bf16[4096,1024]{1,0:T(8,128)(2,1)}, u32[]{:S(2)}, u32[]{:S(2)}) collective-permute-start(bf16[4096,1024]{1,0:T(8,128)(2,1)} %collective-permute-done.refs_2_), channel_id=1, source_target_pairs={{0,1},{1,0},{2,3},{3,2},{4,5},{5,4},{6,7},{7,6}} | collective-permute-start | bytes 25165832 | tf_op jit(solution)/shard_map/ppermute | solution.py:162
  261.6 313.9 %collective-permute-start.4 = (bf16[4096,1024]{1,0:T(8,128)(2,1)}, bf16[4096,1024]{1,0:T(8,128)(2,1)}, u32[]{:S(2)}, u32[]{:S(2)}) collective-permute-start(bf16[4096,1024]{1,0:T(8,128)(2,1)} %refs_0_.3), channel_id=1, source_target_pairs={{0,2},{1,3},{2,0},{3,1},{4,6},{5,7},{6,4},{7,5}} | collective-permute-start | bytes 25165832 | tf_op jit(solution)/shard_map/ppermute | solution.py:162
  261.9 1202.3 %all-gather.24.cloned.1.call-start = ((), (), s32[]{:S(2)}) async-start(), calls=%async_computation.15 | async-start | bytes 4325376 | tf_op jit(solution)/shard_map/all_gather | solution.py:205
  263.4 183.7 %all-to-all-start = ((f32[4,2,16,480]{3,2,1,0:T(8,128)}), f32[4,2,16,480]{3,2,1,0:T(8,128)S(1)}, u32[]{:S(2)}, u32[]{:S(2)}) async-start(f32[4,2,16,480]{3,2,1,0:T(8,128)} %copy.60), calls=%async_computation | async-start | bytes 524288 | tf_op jit(solution)/shard_map/all_to_all | solution.py:189
  266.8 1216.8 %all-gather.22.cloned.1.call-start = ((), (), s32[]{:S(2)}) async-start(), calls=%async_computation.14 | async-start | bytes 4325376 | tf_op jit(solution)/shard_map/all_gather | solution.py:206
  266.9 389.8 %collective-permute-start.3 = (bf16[4096,1024]{1,0:T(8,128)(2,1)}, bf16[4096,1024]{1,0:T(8,128)(2,1)}, u32[]{:S(2)}, u32[]{:S(2)}) collective-permute-start(bf16[4096,1024]{1,0:T(8,128)(2,1)} %refs_0_.3), channel_id=1, source_target_pairs={{0,1},{1,0},{2,3},{3,2},{4,5},{5,4},{6,7},{7,6}} | collective-permute-start | bytes 25165832 | tf_op jit(solution)/shard_map/ppermute | solution.py:162
  267.6 2110.9 %reduce-scatter.11.cloned.1.call-start = ((), (), s32[]{:S(2)}) async-start(), calls=%async_computation.19 | async-start | bytes 34603008 | tf_op jit(solution)/shard_map/reduce_scatter | solution.py:232
  447.2 128.3 %copy-start.4 = (s32[4,1,16,480]{3,2,1,0:T(8,128)}, s32[4,1,16,480]{3,2,1,0:T(8,128)S(1)}, u32[]{:S(2)}) copy-start(s32[4,1,16,480]{3,2,1,0:T(8,128)S(1)} %get-tuple-element.94) | copy-start | bytes 368644
  448.2 3.4 copy-start
  575.5 81.1 %collective-permute-start.5 = (bf16[4096,1024]{1,0:T(8,128)(2,1)}, bf16[4096,1024]{1,0:T(8,128)(2,1)}, u32[]{:S(2)}, u32[]{:S(2)}) collective-permute-start(bf16[4096,1024]{1,0:T(8,128)(2,1)} %collective-permute-done.4.refs_2_), channel_id=1, source_target_pairs={{0,1},{1,0},{2,3},{3,2},{4,5},{5,4},{6,7},{7,6}} | collective-permute-start | bytes 25165832 | tf_op jit(solution)/shard_map/ppermute | solution.py:162
  656.6 3.4 copy-start.1
  1054.6 0.8 copy-start.10
  1054.6 1323.8 %reduce-scatter.13.cloned.1.call-start = ((), (), s32[]{:S(2)}) async-start(), calls=%async_computation.20 | async-start | bytes 34603008 | tf_op jit(solution)/shard_map/reduce_scatter | solution.py:232
  1245.7 1149.8 %reduce-scatter.15.cloned.1.call-start = ((), (), s32[]{:S(2)}) async-start(), calls=%async_computation.21 | async-start | bytes 34603008 | tf_op jit(solution)/shard_map/reduce_scatter | solution.py:233
  1246.3 1149.3 %reduce-scatter.17.cloned.1.call-start = ((), (), s32[]{:S(2)}) async-start(), calls=%async_computation.22 | async-start | bytes 34603008 | tf_op jit(solution)/shard_map/reduce_scatter | solution.py:233
  1284.3 0.9 copy-start.5
  1284.3 1128.4 %reduce-scatter.7.cloned.1.call-start = ((), (), s32[]{:S(2)}) async-start(), calls=%async_computation.17 | async-start | bytes 34603008 | tf_op jit(solution)/shard_map/reduce_scatter | solution.py:231
  1284.9 1342.6 %reduce-scatter.9.cloned.1.call-start = ((), (), s32[]{:S(2)}) async-start(), calls=%async_computation.18 | async-start | bytes 34603008 | tf_op jit(solution)/shard_map/reduce_scatter | solution.py:231
  1444.1 278.4 %collective-permute-start.7 = (f32[32768,128]{1,0:T(8,128)}, f32[32768,128]{1,0:T(8,128)}, u32[]{:S(2)}, u32[]{:S(2)}) collective-permute-start(f32[32768,128]{1,0:T(8,128)} %sum_rows.7), channel_id=1, source_target_pairs={{0,1},{1,0},{2,3},{3,2},{4,5},{5,4},{6,7},{7,6}} | collective-permute-start | bytes 50331656 | tf_op jit(solution)/shard_map/ppermute | solution.py:162
  1625.6 6.3 copy-start.2
  1631.9 17.8 copy-start.8
  1631.9 18.5 copy-start.13
  1631.9 19.2 copy-start.12
  1636.0 7.3 collective-permute-start.10
  1636.0 144.2 %collective-permute-start.9 = (f32[3,2,128,1408]{3,2,1,0:T(8,128)}, f32[3,2,128,1408]{3,2,1,0:T(8,128)}, u32[]{:S(2)}, u32[]{:S(2)}) collective-permute-start(f32[3,2,128,1408]{3,2,1,0:T(8,128)} %get-tuple-element.78), channel_id=1, source_target_pairs={{0,1},{1,0},{2,3},{3,2},{4,5},{5,4},{6,7},{7,6}} | collective-permute-start | bytes 12976136 | tf_op jit(solution)/shard_map/ppermute | solution.py:162
  1649.2 131.0 %collective-permute-start.11 = (f32[3,2,128,1408]{3,2,1,0:T(8,128)}, f32[3,2,128,1408]{3,2,1,0:T(8,128)}, u32[]{:S(2)}, u32[]{:S(2)}) collective-permute-start(f32[3,2,128,1408]{3,2,1,0:T(8,128)} %bitcast_add_fusion), channel_id=1, source_target_pairs={{0,2},{1,3},{2,0},{3,1},{4,6},{5,7},{6,4},{7,5}} | collective-permute-start | bytes 12976136 | tf_op jit(solution)/shard_map/ppermute | solution.py:162
  1687.0 638.8 %collective-permute-start.6 = (f32[32768,128]{1,0:T(8,128)}, f32[32768,128]{1,0:T(8,128)}, u32[]{:S(2)}, u32[]{:S(2)}) collective-permute-start(f32[32768,128]{1,0:T(8,128)} %sum_rows.5), channel_id=1, source_target_pairs={{0,1},{1,0},{2,3},{3,2},{4,5},{5,4},{6,7},{7,6}} | collective-permute-start | bytes 50331656 | tf_op jit(solution)/shard_map/ppermute | solution.py:162
  1740.3 585.4 %collective-permute-start.8 = (f32[32768,128]{1,0:T(8,128)}, f32[32768,128]{1,0:T(8,128)}, u32[]{:S(2)}, u32[]{:S(2)}) collective-permute-start(f32[32768,128]{1,0:T(8,128)} %add.147), channel_id=1, source_target_pairs={{0,2},{1,3},{2,0},{3,1},{4,6},{5,7},{6,4},{7,5}} | collective-permute-start | bytes 50331656 | tf_op jit(solution)/shard_map/ppermute | solution.py:162
  1785.6 2.1 copy-start.3
  1787.8 85.2 %collective-permute-start.12 = (f32[3,128,1408]{2,1,0:T(8,128)S(1)}, f32[3,128,1408]{2,1,0:T(8,128)}, u32[]{:S(2)}, u32[]{:S(2)}) collective-permute-start(f32[3,128,1408]{2,1,0:T(8,128)S(1)} %dynamic-slice_bitcast_fusion.2), channel_id=1, source_target_pairs={{0,4},{4,0},{1,5},{5,1},{2,6},{6,2},{3,7},{7,3}} | collective-permute-start | bytes 6488072 | tf_op jit(solution)/shard_map/ppermute | solution.py:168
  1828.5 344.9 %all-to-all-start.1 = ((f32[4,16,480]{2,1,0:T(8,128)}), f32[4,16,480]{2,1,0:T(8,128)S(1)}, u32[]{:S(2)}, u32[]{:S(2)}) async-start(f32[4,16,480]{2,1,0:T(8,128)} %pad_maximum_fusion.7), calls=%async_computation.1 | async-start | bytes 262144 | tf_op jit(solution)/shard_map/all_to_all | solution.py:251
  1875.5 276.5 %collective-permute-start.14 = (f32[3,128,1408]{2,1,0:T(8,128)S(1)}, f32[3,128,1408]{2,1,0:T(8,128)}, u32[]{:S(2)}, u32[]{:S(2)}) collective-permute-start(f32[3,128,1408]{2,1,0:T(8,128)S(1)} %bitcast_add_fusion.2), channel_id=1, source_target_pairs={{0,2},{1,3},{2,0},{3,1},{4,6},{5,7},{6,4},{7,5}} | collective-permute-start | bytes 6488072 | tf_op jit(solution)/shard_map/ppermute | solution.py:162
  1896.2 277.4 %copy-start.9 = (s32[24576]{0:T(1024)S(1)}, s32[24576]{0:T(1024)}, u32[]{:S(2)}) copy-start(s32[24576]{0:T(1024)} %broadcast_clamp_fusion) | copy-start | bytes 294916
  1896.2 419.2 %collective-permute-start.13 = (f32[3,128,1408]{2,1,0:T(8,128)S(1)}, f32[3,128,1408]{2,1,0:T(8,128)}, u32[]{:S(2)}, u32[]{:S(2)}) collective-permute-start(f32[3,128,1408]{2,1,0:T(8,128)S(1)} %bitcast_add_fusion.2), channel_id=1, source_target_pairs={{0,1},{1,0},{2,3},{3,2},{4,5},{5,4},{6,7},{7,6}} | collective-permute-start | bytes 6488072 | tf_op jit(solution)/shard_map/ppermute | solution.py:162
  2152.0 163.5 %collective-permute-start.15 = (f32[3,128,1408]{2,1,0:T(8,128)}, f32[3,128,1408]{2,1,0:T(8,128)}, u32[]{:S(2)}, u32[]{:S(2)}) collective-permute-start(f32[3,128,1408]{2,1,0:T(8,128)} %collective-permute-done.14), channel_id=1, source_target_pairs={{0,1},{1,0},{2,3},{3,2},{4,5},{5,4},{6,7},{7,6}} | collective-permute-start | bytes 6488072 | tf_op jit(solution)/shard_map/ppermute | solution.py:162
Sparse Core Ops, SparseCore 0:
  17.1 141.8 all-gather.13
  160.6 139.0 all-gather.11
  301.2 139.0 all-gather.9
  442.3 139.0 all-gather.19
  582.7 139.0 all-gather.15
  723.2 139.0 all-gather.17
  863.8 39.1 all-gather.25
  904.5 39.1 all-gather.23
  945.2 39.1 all-gather.21
  1054.7 254.1 reduce-scatter.10
  1311.2 253.9 reduce-scatter.12
  1567.3 283.1 reduce-scatter.14
  1852.8 261.9 reduce-scatter.16
  2116.9 253.9 reduce-scatter.6
  2373.5 253.9 reduce-scatter.8

commit v3 on v2

--- a/solution.py
+++ b/solution.py
@@ -226,7 +226,7 @@
             dw_three = dot32("erd,erf->edf", x_c, dh_three)
             dx_c = (dot32("erf,edf->erd", dh_one, w_a) + dot32("erf,edf->erd", dh_three, w_c)).astype(jnp.bfloat16)
             if c + 1 < CHUNKS:
-                x_rows[c + 1], dy_rows[c + 1], dw_one, dw_two, dw_three, dx_c = tie(x_rows[c + 1], dy_rows[c + 1], dw_one, dw_two, dw_three, dx_c)
+                x_rows[c + 1], dy_rows[c + 1], dx_c = tie(x_rows[c + 1], dy_rows[c + 1], dx_c)
             grads.append((
                 lax.psum_scatter(dw_one, "fsdp", scatter_dimension=1, tiled=True),
                 lax.psum_scatter(dw_two, "fsdp", scatter_dimension=2, tiled=True),

time: 2660 us -> 2600 us (0.977)
  waiting for transfers between devices: 701 us -> 643 us
    reduce_scatter x2, waiting for transfers between devices: 215 us -> 155 us  [device_step(): lax.psum_scatter(dw_one, 'fsdp', scatter_dimension=1, tiled=True)]
  transfers between devices with their start and end apart: 33 -> 33, of which waited for: 5 -> 5; matrix products, arithmetic and copies ran while one was open for 56% -> 57% of each run, Pallas kernels for 15% -> 15%
where the time goes in v3:
time: 2600 us; the launch traced here: 2590 us
  matrix products  958 us (37%)
  waiting for transfers between devices  643 us (25%)
  local copies, waits for them, and re-layouts  423 us (16%)
  Pallas kernels  388 us (15%)
  other arithmetic  148 us (6%)
    dot_general x26, matrix products, dot32(): return jnp.einsum(form, a, b, preferred_element_type=jnp.float32)  958 us
    ppermute x15, waiting for transfers between devices, swap(): return lax.ppermute(value, 'ep', [(i, i ^ bit) for i in range(ep_size)])  253 us
    pallas_call x2, Pallas kernels, gather_rows(): pl.pallas_call(body, grid=(n_src, n_local), in_specs=[pl.BlockSpec((1, 1,...  247 us
    all_to_all x1, waiting for transfers between devices, device_step(): table = lax.all_to_all(table, 'ep', 0, 0, tiled=True)  181 us
    reduce_scatter x2, waiting for transfers between devices, device_step(): lax.psum_scatter(dw_one, 'fsdp', scatter_dimension=1, tiled=True)  155 us
    pallas_call x4, Pallas kernels, sum_rows(): pl.pallas_call(body, grid=(per_chunk,), in_specs=[pl.BlockSpec((1, n_loca...  141 us
    gather x1, local copies, waits for them, and re-layouts, device_step(): jnp.concatenate([dgate, jnp.zeros((1,), jnp.float32)])[slot_idx]  136 us
    scatter x1, local copies, waits for them, and re-layouts, route_slots(): jnp.zeros((n_exp * capacity + 1,), jnp.float32).at[slot_idx]  90.3 us
  transfers between devices with their start and end apart: 33, of which 5 were waited for; matrix products, arithmetic and copies ran while one was open for 57% of the time, Pallas kernels for 15%

profile of v3, /device:TPU:0, one launch (start us, length us, event | category | flops | bytes accessed | tf_op | source)
XLA Modules:
  0.0 2592.3 jit_solution(11126682398373286526)
XLA Ops:
  7.2 9.8 fusion.25
  17.1 9.7 fusion.24
  79.8 90.3 %scatter_custom_fusion.1 = f32[30721]{0:T(1024)S(1)} fusion(s32[24576]{0:T(1024)S(1)} %bitcast.155, f32[24576]{0:T(1024)S(1)} %reshape.222, f32[]{:T(128)} %constant.90.clone.1), kind=kCustom, calls=%fused_computation.79 | custom fusion | bytes 122888 | tf_op jit(solution)/shard_map/scatter | solution.py:28
  170.2 90.3 %scatter_custom_fusion = s32[30721]{0:T(1024)S(1)} fusion(s32[24576]{0:T(1024)S(1)} %bitcast.156, s32[24576]{0:T(1024)S(1)} %add_select_fusion, s32[]{:T(128)} %constant.83.clone.1), kind=kCustom, calls=%fused_computation.81 | custom fusion | bytes 122888 | tf_op jit(solution)/shard_map/scatter | solution.py:27
  265.8 180.6 %all-to-all-done = f32[4,2,16,480]{3,2,1,0:T(8,128)S(1)} async-done(((f32[4,2,16,480]{3,2,1,0:T(8,128)}), f32[4,2,16,480]{3,2,1,0:T(8,128)S(1)}, u32[]{:S(2)}, u32[]{:S(2)}) %all-to-all-start) | async-done | bytes 245792 | tf_op jit(solution)/shard_map/all_to_all | solution.py:189
  450.1 123.7 %gather_rows.2 = (bf16[8,4,480,1024]{3,2,1,0:T(8,128)(2,1)}, bf16[8,4,480,1024]{3,2,1,0:T(8,128)(2,1)}) custom-call(s32[4,1,7680]{2,1,0:T(1,128)S(1)} %convert_element_type.94.tok_ref, bf16[4096,1024]{1,0:T(8,128)(2,1)S(1)} %copy-done, bf16[4096,1024]{1,0:T(8,128)(2,1)} %collective-permute-done.1.refs_1_, bf16[4096,1024]{1,0:T(8,128)(2,1)} %collective-permute-done.refs_2_, ...), custom_call_target="tpu_custom_call" | custom-call | flops 600000000 | bytes 100000000 | tf_op jit(solution)/shard_map/gather_rows/pallas_call | solution.py:78
  575.5 40.8 %fusion.29 = f32[8,1920,704]{1,2,0:T(8,128)} fusion(bf16[8,1920,1024]{2,1,0:T(8,128)(2,1)} %bitcast.170, bf16[8,1024,704]{1,2,0:T(8,128)(2,1)} %all-gather.14.cloned.1.call-done), kind=kOutput, calls=%fused_computation.110 | convolution fusion | flops 22145925120 | bytes 86245376 | tf_op jit(solution)/shard_map/erd,edf->erf/dot_general | solution.py:151
  619.7 123.6 %gather_rows.3 = (bf16[8,4,480,1024]{3,2,1,0:T(8,128)(2,1)}, bf16[8,4,480,1024]{3,2,1,0:T(8,128)(2,1)}) custom-call(s32[4,1,7680]{2,1,0:T(1,128)S(1)} %convert_element_type.94.tok_ref, bf16[4096,1024]{1,0:T(8,128)(2,1)S(1)} %copy-done.1, bf16[4096,1024]{1,0:T(8,128)(2,1)} %collective-permute-done.3.refs_1_, ...), custom_call_target="tpu_custom_call" | custom-call | flops 600000000 | bytes 100000000 | tf_op jit(solution)/shard_map/gather_rows/pallas_call | solution.py:78
  743.3 40.8 %fusion.3 = f32[8,1920,704]{1,2,0:T(8,128)} fusion(bf16[8,704,1024]{2,1,0:T(8,128)(2,1)} %all-gather.10.cloned.1.call-done, bf16[8,1920,1024]{2,1,0:T(8,128)(2,1)} %bitcast.160, f32[8,1920]{1,0:T(8,128)S(1)} %slice.96), kind=kOutput, calls=%fused_computation.20 | convolution fusion | flops 22193111040 | bytes 86306816 | tf_op jit(solution)/shard_map/erd,efd->erf/dot_general | solution.py:151
  784.1 70.6 %select_convert_fusion.1 = (bf16[8,1920,704]{1,2,0:T(8,128)(2,1)}, bf16[8,1920,704]{1,2,0:T(8,128)(2,1)}, bf16[8,1920,704]{1,2,0:T(8,128)(2,1)}) fusion(pred[8,1920]{1,0:T(8,128)(4,1)S(1)} %broadcast_compare_fusion.1, f32[8,1920,704]{1,2,0:T(8,128)} %fusion.29, f32[8,1920,704]{1,2,0:T(8,128)} %fusion.3, bf16[8,1920,1024]{2,1,0:T(8,128)(2,1)} %bitcast.171, ...), kind=kOutput, calls=%fused_computation.10 | convolution fusion | flops 22340567040 | bytes 194395136 | tf_op jit(solution)/shard_map/erd,edf->erf/dot_general | solution.py:151
  854.7 37.9 %fusion.2 = f32[8,704,1024]{2,1,0:T(8,128)} fusion(bf16[8,1920,704]{1,2,0:T(8,128)(2,1)} %get-tuple-element.38, bf16[8,1920,1024]{2,1,0:T(8,128)(2,1)} %bitcast.161, f32[8,1920]{1,0:T(8,128)S(1)} %slice.96), kind=kOutput, calls=%fused_computation.19 | convolution fusion | flops 22193111040 | bytes 76214272 | tf_op jit(solution)/shard_map/erf,erd->efd/dot_general | solution.py:151
  894.2 37.8 %fusion.30 = f32[8,1920,1024]{2,1,0:T(8,128)} fusion(bf16[8,1920,704]{1,2,0:T(8,128)(2,1)} %get-tuple-element.68, bf16[8,1024,704]{1,2,0:T(8,128)(2,1)} %all-gather.14.cloned.1.call-done), kind=kOutput, calls=%fused_computation.111 | convolution fusion | flops 22145925120 | bytes 96075776 | tf_op jit(solution)/shard_map/erf,edf->erd/dot_general | solution.py:151
  932.0 48.4 %add_convert_fusion.1 = bf16[8,1920,1024]{2,1,0:T(8,128)(2,1)} fusion(f32[8,1920,1024]{2,1,0:T(8,128)} %fusion.30, bf16[8,1920,704]{1,2,0:T(8,128)(2,1)} %get-tuple-element.69, bf16[8,1024,704]{1,2,0:T(8,128)(2,1)} %all-gather.12.cloned.1.call-done), kind=kOutput, calls=%fused_computation.5 | convolution fusion | flops 22177382400 | bytes 127533056 | tf_op jit(solution)/shard_map/erf,edf->erd/dot_general | solution.py:151
  980.5 40.8 %fusion.31 = f32[8,1920,704]{1,2,0:T(8,128)} fusion(bf16[8,1920,1024]{2,1,0:T(8,128)(2,1)} %bitcast.166, bf16[8,1024,704]{1,2,0:T(8,128)(2,1)} %all-gather.20.cloned.1.call-done), kind=kOutput, calls=%fused_computation.112 | convolution fusion | flops 22145925120 | bytes 86245376 | tf_op jit(solution)/shard_map/erd,edf->erf/dot_general | solution.py:151
  1021.2 40.8 %fusion.5 = f32[8,1920,704]{1,2,0:T(8,128)} fusion(bf16[8,704,1024]{2,1,0:T(8,128)(2,1)} %all-gather.16.cloned.1.call-done, bf16[8,1920,1024]{2,1,0:T(8,128)(2,1)} %bitcast.163, f32[8,1920]{1,0:T(8,128)S(1)} %slice.101), kind=kOutput, calls=%fused_computation.22 | convolution fusion | flops 22193111040 | bytes 86306816 | tf_op jit(solution)/shard_map/erd,efd->erf/dot_general | solution.py:151
  1062.0 70.7 %select_convert_fusion = (bf16[8,1920,704]{1,2,0:T(8,128)(2,1)}, bf16[8,1920,704]{1,2,0:T(8,128)(2,1)}, bf16[8,1920,704]{1,2,0:T(8,128)(2,1)}) fusion(pred[8,1920]{1,0:T(8,128)(4,1)S(1)} %copy-done.15, f32[8,1920,704]{1,2,0:T(8,128)} %fusion.31, f32[8,1920,704]{1,2,0:T(8,128)} %fusion.5, bf16[8,1920,1024]{2,1,0:T(8,128)(2,1)} %bitcast.167, ...), kind=kOutput, calls=%fused_computation.9 | convolution fusion | flops 22340567040 | bytes 194395136 | tf_op jit(solution)/shard_map/erd,edf->erf/dot_general | solution.py:151
  1132.7 37.9 %fusion.4 = f32[8,704,1024]{2,1,0:T(8,128)} fusion(bf16[8,1920,704]{1,2,0:T(8,128)(2,1)} %get-tuple-element.39, bf16[8,1920,1024]{2,1,0:T(8,128)(2,1)} %bitcast.164, f32[8,1920]{1,0:T(8,128)S(1)} %slice.101), kind=kOutput, calls=%fused_computation.21 | convolution fusion | flops 22193111040 | bytes 76214272 | tf_op jit(solution)/shard_map/erf,erd->efd/dot_general | solution.py:151
  1170.7 37.7 %fusion.40 = f32[8,1024,704]{1,2,0:T(8,128)} fusion(bf16[8,1920,704]{1,2,0:T(8,128)(2,1)} %get-tuple-element.69, bf16[8,1920,1024]{2,1,0:T(8,128)(2,1)} %bitcast.172), kind=kOutput, calls=%fused_computation.121 | convolution fusion | flops 22145925120 | bytes 76152832 | tf_op jit(solution)/shard_map/erd,erf->edf/dot_general | solution.py:151
  1208.5 38.2 %fusion.41 = f32[8,1024,704]{1,2,0:T(8,128)} fusion(bf16[8,1920,704]{1,2,0:T(8,128)(2,1)} %get-tuple-element.66, bf16[8,1920,1024]{2,1,0:T(8,128)(2,1)} %bitcast.168), kind=kOutput, calls=%fused_computation.122 | convolution fusion | flops 22145925120 | bytes 76152832 | tf_op jit(solution)/shard_map/erd,erf->edf/dot_general | solution.py:151
  1246.8 37.9 %fusion.38 = f32[8,1024,704]{1,2,0:T(8,128)} fusion(bf16[8,1920,704]{1,2,0:T(8,128)(2,1)} %get-tuple-element.68, bf16[8,1920,1024]{2,1,0:T(8,128)(2,1)} %bitcast.173), kind=kOutput, calls=%fused_computation.119 | convolution fusion | flops 22145925120 | bytes 76152832 | tf_op jit(solution)/shard_map/erd,erf->edf/dot_general | solution.py:151
  1287.7 37.6 %fusion.32 = f32[8,1920,1024]{2,1,0:T(8,128)} fusion(bf16[8,1920,704]{1,2,0:T(8,128)(2,1)} %get-tuple-element.65, bf16[8,1024,704]{1,2,0:T(8,128)(2,1)} %all-gather.20.cloned.1.call-done), kind=kOutput, calls=%fused_computation.113 | convolution fusion | flops 22145925120 | bytes 96075776 | tf_op jit(solution)/shard_map/erf,edf->erd/dot_general | solution.py:151
  1325.3 48.4 %add_convert_fusion = bf16[8,1920,1024]{2,1,0:T(8,128)(2,1)} fusion(f32[8,1920,1024]{2,1,0:T(8,128)} %fusion.32, bf16[8,1920,704]{1,2,0:T(8,128)(2,1)} %get-tuple-element.66, bf16[8,1024,704]{1,2,0:T(8,128)(2,1)} %all-gather.18.cloned.1.call-done), kind=kOutput, calls=%fused_computation.3 | convolution fusion | flops 22177382400 | bytes 127533056 | tf_op jit(solution)/shard_map/erf,edf->erd/dot_general | solution.py:151
  1373.7 35.2 %sum_rows.4 = f32[32768,128]{1,0:T(8,128)} custom-call(s32[1,7680]{1,0:T(1,128)} %reshape_squeeze.12.tok_ref, bf16[8,4,480,1024]{3,2,1,0:T(8,128)(2,1)} %bitcast.138, bf16[8,4,480,1024]{3,2,1,0:T(8,128)(2,1)} %bitcast.142), custom_call_target="tpu_custom_call" | custom-call | flops 150000000 | bytes 32000000 | tf_op jit(solution)/shard_map/sum_rows/pallas_call | solution.py:130
  1408.9 35.2 %sum_rows.7 = f32[32768,128]{1,0:T(8,128)} custom-call(s32[1,7680]{1,0:T(1,128)} %reshape_squeeze.15.tok_ref, bf16[8,4,480,1024]{3,2,1,0:T(8,128)(2,1)} %bitcast.139, bf16[8,4,480,1024]{3,2,1,0:T(8,128)(2,1)} %bitcast.143), custom_call_target="tpu_custom_call" | custom-call | flops 150000000 | bytes 32000000 | tf_op jit(solution)/shard_map/sum_rows/pallas_call | solution.py:130
  1444.6 19.6 fusion.34
  1464.2 19.5 fusion.33
  1483.7 33.7 %multiply_convert_fusion.7 = (bf16[4096,1408]{1,0:T(8,128)(2,1)}, bf16[4096,1408]{1,0:T(8,128)(2,1)}) fusion(f32[4096,1408]{1,0:T(8,128)} %fusion.34, f32[4096,1408]{1,0:T(8,128)} %fusion.33, bf16[4096,1024]{1,0:T(8,128)(2,1)} %refs_0_.3, bf16[1408,1024]{1,0:T(8,128)(2,1)} %all-gather.22.cloned.1.call-done), kind=kOutput, calls=%fused_computation.27 | convolution fusion | flops 11886133248 | bytes 80478208 | tf_op jit(solution)/shard_map/td,fd->tf/dot_general | solution.py:151
  1517.4 19.6 fusion.37
  1537.0 37.9 %fusion.39 = f32[8,1024,704]{1,2,0:T(8,128)} fusion(bf16[8,1920,704]{1,2,0:T(8,128)(2,1)} %get-tuple-element.65, bf16[8,1920,1024]{2,1,0:T(8,128)(2,1)} %bitcast.169), kind=kOutput, calls=%fused_computation.120 | convolution fusion | flops 22145925120 | bytes 76152832 | tf_op jit(solution)/shard_map/erd,erf->edf/dot_general | solution.py:151
  1574.9 19.5 fusion.36
  1594.4 24.6 fusion.7
  1651.8 35.2 %sum_rows.5 = f32[32768,128]{1,0:T(8,128)} custom-call(s32[1,7680]{1,0:T(1,128)} %reshape_squeeze.13.tok_ref, bf16[8,4,480,1024]{3,2,1,0:T(8,128)(2,1)} %bitcast.140, bf16[8,4,480,1024]{3,2,1,0:T(8,128)(2,1)} %bitcast.144), custom_call_target="tpu_custom_call" | custom-call | flops 150000000 | bytes 32000000 | tf_op jit(solution)/shard_map/sum_rows/pallas_call | solution.py:130
  1687.0 35.6 %sum_rows.6 = f32[32768,128]{1,0:T(8,128)} custom-call(s32[1,7680]{1,0:T(1,128)} %reshape_squeeze.14.tok_ref, bf16[8,4,480,1024]{3,2,1,0:T(8,128)(2,1)} %bitcast.141, bf16[8,4,480,1024]{3,2,1,0:T(8,128)(2,1)} %bitcast.145), custom_call_target="tpu_custom_call" | custom-call | flops 150000000 | bytes 32000000 | tf_op jit(solution)/shard_map/sum_rows/pallas_call | solution.py:130
  1722.6 17.8 add.147
  1742.0 38.3 %multiply_reduce_fusion = f32[8,1920]{1,0:T(8,128)S(1)} fusion(bf16[8,1920,704]{1,2,0:T(8,128)(2,1)} %get-tuple-element.39, bf16[8,1920,1024]{2,1,0:T(8,128)(2,1)} %bitcast.165, bf16[8,704,1024]{2,1,0:T(8,128)(2,1)} %all-gather.16.cloned.1.call-done), kind=kOutput, calls=%fused_computation.7 | convolution fusion | flops 22178349056 | bytes 64679936 | tf_op jit(solution)/shard_map/erd,efd->erf/dot_general | solution.py:151
  1789.4 38.2 %multiply_reduce_fusion.1 = f32[8,1920]{1,0:T(8,128)S(1)} fusion(bf16[8,1920,704]{1,2,0:T(8,128)(2,1)} %get-tuple-element.38, bf16[8,1920,1024]{2,1,0:T(8,128)(2,1)} %bitcast.162, bf16[8,704,1024]{2,1,0:T(8,128)(2,1)} %all-gather.10.cloned.1.call-done), kind=kOutput, calls=%fused_computation.8 | convolution fusion | flops 22178349056 | bytes 64679936 | tf_op jit(solution)/shard_map/erd,efd->erf/dot_general | solution.py:151
  1832.1 51.7 %collective-permute-done.12 = f32[3,128,1408]{2,1,0:T(8,128)} collective-permute-done((f32[3,128,1408]{2,1,0:T(8,128)S(1)}, f32[3,128,1408]{2,1,0:T(8,128)}, u32[]{:S(2)}, u32[]{:S(2)}) %collective-permute-start.12) | collective-permute-done | bytes 2162720 | tf_op jit(solution)/shard_map/ppermute | solution.py:168
  1886.8 19.2 fusion.35
  1906.0 246.0 %collective-permute-done.14 = f32[3,128,1408]{2,1,0:T(8,128)} collective-permute-done((f32[3,128,1408]{2,1,0:T(8,128)S(1)}, f32[3,128,1408]{2,1,0:T(8,128)}, u32[]{:S(2)}, u32[]{:S(2)}) %collective-permute-start.14) | collective-permute-done | bytes 2162720 | tf_op jit(solution)/shard_map/ppermute | solution.py:162
  2152.0 21.4 add_convert_fusion.3
  2173.6 135.5 %gather_fusion = f32[24576]{0:T(1024)S(1)} fusion(f32[30721]{0:T(1024)S(1)} %pad_maximum_fusion.8, s32[24576]{0:T(1024)S(1)} %copy-done.10), kind=kCustom, calls=%fused_computation | custom fusion | bytes 294912 | tf_op jit(solution)/shard_map/gather | solution.py:252
  2325.8 22.7 add_add_fusion
  2348.5 18.0 reshape.198
  2366.5 12.0 add_convert_fusion.2
  2378.5 17.1 pad_maximum_fusion.1
  2395.6 17.1 pad_maximum_fusion.2
  2412.8 155.5 %reduce-scatter.9.cloned.1.call-done = f32[8,512,704]{1,2,0:T(8,128)} async-done(((f32[8,1024,704]{1,2,0:T(8,128)}), f32[8,512,704]{1,2,0:T(8,128)}) %reduce-scatter.9.cloned.1.call-update) | async-done | bytes 11534352 | tf_op jit(solution)/shard_map/reduce_scatter | solution.py:231
  2568.2 17.1 pad_maximum_fusion
  (178 shorter events, 139.9 us)
Async XLA Ops:
  7.2 568.3 %all-gather.14.cloned.1.call-start = ((), (), s32[]{:S(2)}) async-start(), calls=%async_computation.10 | async-start | bytes 17301504 | tf_op jit(solution)/shard_map/all_gather | solution.py:200
  17.0 726.2 %all-gather.10.cloned.1.call-start = ((), (), s32[]{:S(2)}) async-start(), calls=%async_computation.8 | async-start | bytes 17301504 | tf_op jit(solution)/shard_map/all_gather | solution.py:202
  26.8 757.3 %all-gather.12.cloned.1.call-start = ((), (), s32[]{:S(2)}) async-start(), calls=%async_computation.9 | async-start | bytes 17301504 | tf_op jit(solution)/shard_map/all_gather | solution.py:201
  36.4 4.7 copy-start.7
  36.4 11.1 copy-start.12
  36.5 944.0 %all-gather.20.cloned.1.call-start = ((), (), s32[]{:S(2)}) async-start(), calls=%async_computation.13 | async-start | bytes 17301504 | tf_op jit(solution)/shard_map/all_gather | solution.py:200
  37.0 984.2 %all-gather.16.cloned.1.call-start = ((), (), s32[]{:S(2)}) async-start(), calls=%async_computation.11 | async-start | bytes 17301504 | tf_op jit(solution)/shard_map/all_gather | solution.py:202
  37.6 1024.4 %all-gather.18.cloned.1.call-start = ((), (), s32[]{:S(2)}) async-start(), calls=%async_computation.12 | async-start | bytes 17301504 | tf_op jit(solution)/shard_map/all_gather | solution.py:201
  37.7 409.0 %collective-permute-start.1 = (bf16[4096,1024]{1,0:T(8,128)(2,1)}, bf16[4096,1024]{1,0:T(8,128)(2,1)}, u32[]{:S(2)}, u32[]{:S(2)}) collective-permute-start(bf16[4096,1024]{1,0:T(8,128)(2,1)} %refs_0_.2), channel_id=1, source_target_pairs={{0,1},{1,0},{2,3},{3,2},{4,5},{5,4},{6,7},{7,6}} | collective-permute-start | bytes 25165832 | tf_op jit(solution)/shard_map/ppermute | solution.py:162
  38.5 222.1 %collective-permute-start = (bf16[4096,1024]{1,0:T(8,128)(2,1)}, bf16[4096,1024]{1,0:T(8,128)(2,1)}, u32[]{:S(2)}, u32[]{:S(2)}) collective-permute-start(bf16[4096,1024]{1,0:T(8,128)(2,1)} %refs_0_.2), channel_id=1, source_target_pairs={{0,2},{1,3},{2,0},{3,1},{4,6},{5,7},{6,4},{7,5}} | collective-permute-start | bytes 25165832 | tf_op jit(solution)/shard_map/ppermute | solution.py:162
  41.1 1403.5 %all-gather.26.cloned.1.call-start = ((), (), s32[]{:S(2)}) async-start(), calls=%async_computation.16 | async-start | bytes 4325376 | tf_op jit(solution)/shard_map/all_gather | solution.py:204
  51.1 3.4 copy-start.3
  79.8 180.7 %copy-start.8 = (s32[24576,1]{0,1:T(1,128)}, s32[24576,1]{0,1:T(1,128)S(1)}, u32[]{:S(2)}) copy-start(s32[24576,1]{0,1:T(1,128)S(1)} %compare_select_fusion) | copy-start | bytes 294916
  260.7 186.0 %collective-permute-start.2 = (bf16[4096,1024]{1,0:T(8,128)(2,1)}, bf16[4096,1024]{1,0:T(8,128)(2,1)}, u32[]{:S(2)}, u32[]{:S(2)}) collective-permute-start(bf16[4096,1024]{1,0:T(8,128)(2,1)} %collective-permute-done.refs_2_), channel_id=1, source_target_pairs={{0,1},{1,0},{2,3},{3,2},{4,5},{5,4},{6,7},{7,6}} | collective-permute-start | bytes 25165832 | tf_op jit(solution)/shard_map/ppermute | solution.py:162
  260.9 312.9 %collective-permute-start.4 = (bf16[4096,1024]{1,0:T(8,128)(2,1)}, bf16[4096,1024]{1,0:T(8,128)(2,1)}, u32[]{:S(2)}, u32[]{:S(2)}) collective-permute-start(bf16[4096,1024]{1,0:T(8,128)(2,1)} %refs_0_.3), channel_id=1, source_target_pairs={{0,2},{1,3},{2,0},{3,1},{4,6},{5,7},{6,4},{7,5}} | collective-permute-start | bytes 25165832 | tf_op jit(solution)/shard_map/ppermute | solution.py:162
  261.9 184.4 %all-to-all-start = ((f32[4,2,16,480]{3,2,1,0:T(8,128)}), f32[4,2,16,480]{3,2,1,0:T(8,128)S(1)}, u32[]{:S(2)}, u32[]{:S(2)}) async-start(f32[4,2,16,480]{3,2,1,0:T(8,128)} %copy.60), calls=%async_computation | async-start | bytes 524288 | tf_op jit(solution)/shard_map/all_to_all | solution.py:189
  265.4 1198.8 %all-gather.24.cloned.1.call-start = ((), (), s32[]{:S(2)}) async-start(), calls=%async_computation.15 | async-start | bytes 4325376 | tf_op jit(solution)/shard_map/all_gather | solution.py:205
  265.4 350.9 %collective-permute-start.3 = (bf16[4096,1024]{1,0:T(8,128)(2,1)}, bf16[4096,1024]{1,0:T(8,128)(2,1)}, u32[]{:S(2)}, u32[]{:S(2)}) collective-permute-start(bf16[4096,1024]{1,0:T(8,128)(2,1)} %refs_0_.3), channel_id=1, source_target_pairs={{0,1},{1,0},{2,3},{3,2},{4,5},{5,4},{6,7},{7,6}} | collective-permute-start | bytes 25165832 | tf_op jit(solution)/shard_map/ppermute | solution.py:162
  446.5 127.3 %copy-start.5 = (s32[4,1,16,480]{3,2,1,0:T(8,128)}, s32[4,1,16,480]{3,2,1,0:T(8,128)S(1)}, u32[]{:S(2)}) copy-start(s32[4,1,16,480]{3,2,1,0:T(8,128)S(1)} %get-tuple-element.88) | copy-start | bytes 368644
  446.7 3.4 copy-start
  573.8 42.5 %collective-permute-start.5 = (bf16[4096,1024]{1,0:T(8,128)(2,1)}, bf16[4096,1024]{1,0:T(8,128)(2,1)}, u32[]{:S(2)}, u32[]{:S(2)}) collective-permute-start(bf16[4096,1024]{1,0:T(8,128)(2,1)} %collective-permute-done.4.refs_2_), channel_id=1, source_target_pairs={{0,1},{1,0},{2,3},{3,2},{4,5},{5,4},{6,7},{7,6}} | collective-permute-start | bytes 25165832 | tf_op jit(solution)/shard_map/ppermute | solution.py:162
  573.9 909.8 %all-gather.22.cloned.1.call-start = ((), (), s32[]{:S(2)}) async-start(), calls=%async_computation.14 | async-start | bytes 4325376 | tf_op jit(solution)/shard_map/all_gather | solution.py:206
  574.6 1803.9 %reduce-scatter.11.cloned.1.call-start = ((), (), s32[]{:S(2)}) async-start(), calls=%async_computation.19 | async-start | bytes 34603008 | tf_op jit(solution)/shard_map/reduce_scatter | solution.py:232
  616.3 3.4 copy-start.1
  892.6 1485.8 %reduce-scatter.13.cloned.1.call-start = ((), (), s32[]{:S(2)}) async-start(), calls=%async_computation.20 | async-start | bytes 34603008 | tf_op jit(solution)/shard_map/reduce_scatter | solution.py:232
  1021.2 40.8 %copy-start.15 = (pred[8,1920]{1,0:T(8,128)(4,1)S(1)}, pred[8,1920]{1,0:T(8,128)(4,1)}, u32[]{:S(2)}) copy-start(pred[8,1920]{1,0:T(8,128)(4,1)} %broadcast_compare_fusion) | copy-start | bytes 46084
  1170.7 1225.0 %reduce-scatter.15.cloned.1.call-start = ((), (), s32[]{:S(2)}) async-start(), calls=%async_computation.21 | async-start | bytes 34603008 | tf_op jit(solution)/shard_map/reduce_scatter | solution.py:233
  1208.5 1187.2 %reduce-scatter.17.cloned.1.call-start = ((), (), s32[]{:S(2)}) async-start(), calls=%async_computation.22 | async-start | bytes 34603008 | tf_op jit(solution)/shard_map/reduce_scatter | solution.py:233
  1246.8 1166.0 %reduce-scatter.7.cloned.1.call-start = ((), (), s32[]{:S(2)}) async-start(), calls=%async_computation.17 | async-start | bytes 34603008 | tf_op jit(solution)/shard_map/reduce_scatter | solution.py:231
  1284.7 0.9 copy-start.6
  1284.8 1283.5 %reduce-scatter.9.cloned.1.call-start = ((), (), s32[]{:S(2)}) async-start(), calls=%async_computation.18 | async-start | bytes 34603008 | tf_op jit(solution)/shard_map/reduce_scatter | solution.py:231
  1444.1 278.5 %collective-permute-start.7 = (f32[32768,128]{1,0:T(8,128)}, f32[32768,128]{1,0:T(8,128)}, u32[]{:S(2)}, u32[]{:S(2)}) collective-permute-start(f32[32768,128]{1,0:T(8,128)} %sum_rows.7), channel_id=1, source_target_pairs={{0,1},{1,0},{2,3},{3,2},{4,5},{5,4},{6,7},{7,6}} | collective-permute-start | bytes 50331656 | tf_op jit(solution)/shard_map/ppermute | solution.py:162
  1625.6 6.3 copy-start.2
  1631.9 17.8 copy-start.9
  1631.9 18.5 copy-start.14
  1631.9 19.2 copy-start.13
  1636.0 7.3 collective-permute-start.10
  1636.1 144.2 %collective-permute-start.9 = (f32[3,2,128,1408]{3,2,1,0:T(8,128)}, f32[3,2,128,1408]{3,2,1,0:T(8,128)}, u32[]{:S(2)}, u32[]{:S(2)}) collective-permute-start(f32[3,2,128,1408]{3,2,1,0:T(8,128)} %get-tuple-element.72), channel_id=1, source_target_pairs={{0,1},{1,0},{2,3},{3,2},{4,5},{5,4},{6,7},{7,6}} | collective-permute-start | bytes 12976136 | tf_op jit(solution)/shard_map/ppermute | solution.py:162
  1649.3 131.0 %collective-permute-start.11 = (f32[3,2,128,1408]{3,2,1,0:T(8,128)}, f32[3,2,128,1408]{3,2,1,0:T(8,128)}, u32[]{:S(2)}, u32[]{:S(2)}) collective-permute-start(f32[3,2,128,1408]{3,2,1,0:T(8,128)} %bitcast_add_fusion), channel_id=1, source_target_pairs={{0,2},{1,3},{2,0},{3,1},{4,6},{5,7},{6,4},{7,5}} | collective-permute-start | bytes 12976136 | tf_op jit(solution)/shard_map/ppermute | solution.py:162
  1687.0 638.8 %collective-permute-start.6 = (f32[32768,128]{1,0:T(8,128)}, f32[32768,128]{1,0:T(8,128)}, u32[]{:S(2)}, u32[]{:S(2)}) collective-permute-start(f32[32768,128]{1,0:T(8,128)} %sum_rows.5), channel_id=1, source_target_pairs={{0,1},{1,0},{2,3},{3,2},{4,5},{5,4},{6,7},{7,6}} | collective-permute-start | bytes 50331656 | tf_op jit(solution)/shard_map/ppermute | solution.py:162
  1740.4 585.4 %collective-permute-start.8 = (f32[32768,128]{1,0:T(8,128)}, f32[32768,128]{1,0:T(8,128)}, u32[]{:S(2)}, u32[]{:S(2)}) collective-permute-start(f32[32768,128]{1,0:T(8,128)} %add.147), channel_id=1, source_target_pairs={{0,2},{1,3},{2,0},{3,1},{4,6},{5,7},{6,4},{7,5}} | collective-permute-start | bytes 50331656 | tf_op jit(solution)/shard_map/ppermute | solution.py:162
  1785.6 2.1 copy-start.4
  1787.8 96.0 %collective-permute-start.12 = (f32[3,128,1408]{2,1,0:T(8,128)S(1)}, f32[3,128,1408]{2,1,0:T(8,128)}, u32[]{:S(2)}, u32[]{:S(2)}) collective-permute-start(f32[3,128,1408]{2,1,0:T(8,128)S(1)} %dynamic-slice_bitcast_fusion.2), channel_id=1, source_target_pairs={{0,4},{4,0},{1,5},{5,1},{2,6},{6,2},{3,7},{7,3}} | collective-permute-start | bytes 6488072 | tf_op jit(solution)/shard_map/ppermute | solution.py:168
  1828.6 344.9 %all-to-all-start.1 = ((f32[4,16,480]{2,1,0:T(8,128)}), f32[4,16,480]{2,1,0:T(8,128)S(1)}, u32[]{:S(2)}, u32[]{:S(2)}) async-start(f32[4,16,480]{2,1,0:T(8,128)} %pad_maximum_fusion.7), calls=%async_computation.1 | async-start | bytes 262144 | tf_op jit(solution)/shard_map/all_to_all | solution.py:251
  1886.3 265.7 %collective-permute-start.14 = (f32[3,128,1408]{2,1,0:T(8,128)S(1)}, f32[3,128,1408]{2,1,0:T(8,128)}, u32[]{:S(2)}, u32[]{:S(2)}) collective-permute-start(f32[3,128,1408]{2,1,0:T(8,128)S(1)} %bitcast_add_fusion.2), channel_id=1, source_target_pairs={{0,2},{1,3},{2,0},{3,1},{4,6},{5,7},{6,4},{7,5}} | collective-permute-start | bytes 6488072 | tf_op jit(solution)/shard_map/ppermute | solution.py:162
  1906.0 267.6 %copy-start.10 = (s32[24576]{0:T(1024)S(1)}, s32[24576]{0:T(1024)}, u32[]{:S(2)}) copy-start(s32[24576]{0:T(1024)} %broadcast_clamp_fusion) | copy-start | bytes 294916
  1906.0 409.5 %collective-permute-start.13 = (f32[3,128,1408]{2,1,0:T(8,128)S(1)}, f32[3,128,1408]{2,1,0:T(8,128)}, u32[]{:S(2)}, u32[]{:S(2)}) collective-permute-start(f32[3,128,1408]{2,1,0:T(8,128)S(1)} %bitcast_add_fusion.2), channel_id=1, source_target_pairs={{0,1},{1,0},{2,3},{3,2},{4,5},{5,4},{6,7},{7,6}} | collective-permute-start | bytes 6488072 | tf_op jit(solution)/shard_map/ppermute | solution.py:162
  2152.0 163.5 %collective-permute-start.15 = (f32[3,128,1408]{2,1,0:T(8,128)}, f32[3,128,1408]{2,1,0:T(8,128)}, u32[]{:S(2)}, u32[]{:S(2)}) collective-permute-start(f32[3,128,1408]{2,1,0:T(8,128)} %collective-permute-done.14), channel_id=1, source_target_pairs={{0,1},{1,0},{2,3},{3,2},{4,5},{5,4},{6,7},{7,6}} | collective-permute-start | bytes 6488072 | tf_op jit(solution)/shard_map/ppermute | solution.py:162
  (1 other events, 0.8 us)
Sparse Core Ops, SparseCore 0:
  17.1 141.8 all-gather.13
  160.6 139.0 all-gather.9
  301.2 139.0 all-gather.11
  442.3 139.0 all-gather.19
  582.7 139.0 all-gather.15
  723.2 139.0 all-gather.17
  863.8 39.1 all-gather.25
  904.5 39.1 all-gather.23
  945.2 39.1 all-gather.21
  986.5 253.9 reduce-scatter.10
  1242.7 253.9 reduce-scatter.12
  1498.9 253.9 reduce-scatter.14
  1755.1 300.2 reduce-scatter.16
  2057.6 253.9 reduce-scatter.6
  2314.2 253.9 reduce-scatter.8
